TPU v7x, 128 devices: a whole 4x4x4 slice. The times are simulated.
128 devices in a mesh: samp: 64 (over x, y, z), tp: 2 (over core).
Axes of the slice: x: 4, y: 4, z: 4, core: 2. Of those that a mesh axis runs over, the one named last changes fastest.
Arguments:
- images: bfloat16 [128, 12288], P(None, 'tp'), may hold values from -6 to 6
- enc_mean: float32 [128, 128], replicated, may hold values from -0.3 to 0.3
- enc_logscale: float32 [128, 128], replicated, may hold values from -0.15 to 0
- noise: float32 [128, 512, 128], P(None, 'samp'), may hold values from -5 to 5
- w_in: bfloat16 [128, 1024], P(None, 'tp'), may hold values from -0.5 to 0.5
- b_in: bfloat16 [1, 1024], P(None, 'tp'), may hold values from -3 to 3
- w_out: bfloat16 [1024, 12288], P(None, 'tp'), may hold values from -0.0078125 to 0.0078125
- b_out: float32 [1, 12288], P(None, 'tp'), may hold values from -3 to 3
- pixel_logscale: float32 [1, 12288], P(None, 'tp'), may hold values from 0 to 1
Outputs:
- bound: float32 [128], replicated
- log_weights: float32 [128, 512], P(None, 'samp')
All inputs are finite; a program needn't handle non-finite values.
Results may differ from a plain program's by a relative error of at most 0.00073.
Values may be sent and summed in bfloat16 or wider, within the bound.
A program may use at most 64 MiB of HBM per device.

v0:
```python
import math

import jax
import jax.numpy as jnp
from jax import lax
from jax.sharding import PartitionSpec as P

HALF_LOG_TAU = 0.9189385332046727


def side_by_side(arrays, axis, dim, along):
    ends, at = ([], 0)
    for a in arrays[:-1]:
        at += a.shape[along]
        ends.append(at)
    both = jnp.concatenate(arrays, axis=along)
    return tuple(jnp.split(lax.all_gather(both, axis, axis=dim, tiled=True), ends, axis=along))


def over_pieces(shard, axis):
    return lax.all_gather(shard, axis).sum(0)


def from_everyone(shard, axis):
    length = lax.axis_size(axis)
    return lax.all_to_all(
        jnp.broadcast_to(shard[None], (length, *shard.shape)), axis, 0, 0, tiled=True
    )


def all_in_one(shard, axis):
    leaves = jax.tree.leaves(shard)
    order = sorted(range(len(leaves)), key=lambda k: -leaves[k].size)
    width = (1, *leaves[order[0]].shape)[-1]
    lines = [
        jnp.pad(leaves[k].reshape(-1), (0, -leaves[k].size % width)).reshape(-1, width)
        for k in order
    ]
    both, at, found = (from_everyone(jnp.concatenate(lines), axis), 0, {})
    for k, line in zip(order, lines):
        piece = both[:, at : at + len(line)].reshape(len(both), -1)
        found[k] = piece[:, : leaves[k].size].reshape(-1, *leaves[k].shape)
        at += len(line)
    numbers = iter(range(len(leaves)))
    return jax.tree.map(lambda _: found[next(numbers)], shard)


def joined_by_halves(pieces, combine):
    while len(jax.tree.leaves(pieces)[0]) > 1:
        pieces = jax.vmap(combine)(
            *(jax.tree.map(lambda part: part[side::2], pieces) for side in (0, 1))
        )
    return jax.tree.map(lambda part: part[0], pieces)


def joined_all(shard, axis, combine):
    pieces = all_in_one(shard, axis)
    return joined_by_halves(pieces, combine)


def combine_lse(first, second):
    highest = jnp.maximum(first[0], second[0])
    return (
        highest,
        first[1] * jnp.exp(first[0] - highest) + second[1] * jnp.exp(second[0] - highest),
    )


def on_device(images, enc_mean, enc_logscale, noise, w_in, b_in, w_out, b_out, pixel_logscale):
    image_count, sample_count, latent_dims = noise.shape
    latent = enc_mean[:, None, :] + jnp.exp(enc_logscale)[:, None, :] * noise
    latent_rows = latent.reshape(image_count * sample_count, latent_dims).astype(jnp.bfloat16)
    w_whole, b_whole = side_by_side((w_in, b_in), "tp", 1, 0)
    hidden = jax.nn.relu(
        jnp.dot(latent_rows, w_whole, preferred_element_type=jnp.float32)
        + b_whole.astype(jnp.float32)
    ).astype(jnp.bfloat16)
    pixel_share = images.shape[1]
    all_pixels = pixel_share * lax.axis_size("tp")
    piece_width = math.gcd(pixel_share, 1024)
    piece_count = pixel_share // piece_width
    inverse = jnp.exp(-pixel_logscale)
    share_constant = -jnp.sum(pixel_logscale) - pixel_share * HALF_LOG_TAU

    def add_piece(position, running):
        offset = position * piece_width
        w_piece = lax.dynamic_slice_in_dim(w_out, offset, piece_width, 1)
        bias_piece = lax.dynamic_slice_in_dim(b_out, offset, piece_width, 1)
        inverse_piece = lax.dynamic_slice_in_dim(inverse, offset, piece_width, 1)
        image_piece = lax.dynamic_slice_in_dim(images, offset, piece_width, 1)
        pixel_mean = jnp.dot(hidden, w_piece, preferred_element_type=jnp.float32) + bias_piece
        pixel_mean = pixel_mean.reshape(image_count, sample_count, piece_width)
        scaled = (image_piece[:, None, :].astype(jnp.float32) - pixel_mean) * inverse_piece[
            None, :, :
        ]
        return running + jnp.sum(-0.5 * scaled * scaled, axis=2)

    partial_loglik = (
        lax.fori_loop(
            0, piece_count, add_piece, jnp.zeros((image_count, sample_count), jnp.float32)
        )
        + share_constant
    )
    prior = jnp.sum(-0.5 * latent * latent - HALF_LOG_TAU, axis=2)
    posterior = jnp.sum(-0.5 * noise * noise - enc_logscale[:, None, :] - HALF_LOG_TAU, axis=2)
    loglik = over_pieces(partial_loglik, "tp")
    logw = loglik + prior - posterior
    local_peak = jnp.max(logw, axis=1)
    local_sum = jnp.sum(jnp.exp(logw - local_peak[:, None]), axis=1)
    peak, sum_exp = joined_all((local_peak, local_sum), "samp", combine_lse)
    all_samples = sample_count * lax.axis_size("samp")
    bound = (peak + jnp.log(sum_exp) - jnp.log(jnp.float32(all_samples))) / all_pixels
    log_weights = (
        logw - peak[:, None] - jnp.log(sum_exp)[:, None] + jnp.log(jnp.float32(all_samples))
    )
    return (bound, log_weights)


def solution(mesh):
    in_specs = (
        P(None, "tp"),
        P(),
        P(),
        P(None, "samp", None),
        P(None, "tp"),
        P(None, "tp"),
        P(None, "tp"),
        P(None, "tp"),
        P(None, "tp"),
    )
    out_specs = (P(), P(None, "samp"))
    return jax.shard_map(
        on_device, mesh=mesh, in_specs=in_specs, out_specs=out_specs, check_vma=False
    )
```

profile of v0, /device:TPU:1, one launch (start us, length us, event | category | flops | bytes accessed | tf_op | source)
XLA Modules:
  0.0 127.2 jit_solution(10380896752700722803)
XLA Ops:
  0.6 0.0 copy-start
  0.6 0.9 pad_maximum_fusion
  1.6 3.0 %all_gather.9 = bf16[129,1024]{1,0:T(8,128)(2,1)S(1)} all-gather(bf16[129,512]{1,0:T(8,128)(2,1)S(1)} %pad_maximum_fusion), channel_id=1, replica_groups=mesh['samp'=64,'tp'=2] {'tp'}, dimensions={1}, use_global_device_ids=true | all-gather | bytes 396288 | tf_op jit(solution)/shard_map/all_gather | solution.py:17
  4.6 0.9 exp.45
  5.5 1.5 %fusion.8 = (f32[128,8]{1,0:T(8,128)S(1)}, f32[128,8]{1,0:T(8,128)S(1)}) fusion(f32[128,8,128]{2,1,0:T(8,128)} %param.14, f32[128,128]{1,0:T(8,128)S(1)} %exp.45, f32[128,128]{1,0:T(8,128)} %param.12, f32[128,128]{1,0:T(8,128)} %param.13), kind=kLoop, calls=%fused_computation.16 | loop fusion | flops 1439744 | bytes 729088 | tf_op jit(solution)/shard_map/reduce_sum | solution.py:104
  6.9 1.8 %maximum_convert_fusion = bf16[1024,1024]{1,0:T(8,128)(2,1)S(1)} fusion(f32[1024]{0:T(1024)S(1)} %bitcast.46, f32[128,8,128]{2,1,0:T(8,128)} %param.14, bf16[129,1024]{1,0:T(8,128)(2,1)S(1)} %all_gather.9, f32[128,128]{1,0:T(8,128)S(1)} %exp.45, f32[128,128]{1,0:T(8,128)} %param.12), kind=kOutput, calls=%fused_computation.12 | convolution fusion | flops 271974400 | bytes 3018752 | tf_op jit(solution)/shard_map/dot_general | solution.py:75
  8.7 0.0 copy-done
  8.7 0.7 fusion.20
  9.4 93.5 %while.14 = (s32[]{:T(128)}, f32[128,8]{1,0:T(8,128)S(1)}, bf16[128,6144]{1,0:T(8,128)(2,1)}, bf16[1024,6144]{1,0:T(8,128)(2,1)}, bf16[1024,1024]{1,0:T(8,128)(2...) while((s32[]{:T(128)}, f32[128,8]{1,0:T(8,128)S(1)}, ...), condition=%wide.region_2.0_spmd.clone, body=%wide.region_0.0_spmd.clone.sunk | while | flops 2153907200 | bytes 22331568 | solution.py:99
  9.4 0.7 constant_dynamic-slice_fusion.3
  10.0 1.0 dynamic-slice_convert_fusion.2
  11.0 2.5 %broadcast_bitcast_fusion.2 = f32[1024,1024]{1,0:T(8,128)} fusion(f32[128,1024]{1,0:T(8,128)S(1)} %dynamic-slice_convert_fusion.2), kind=kLoop, calls=%fused_computation.6.clone.1 | loop fusion | bytes 4718592 | tf_op jit(solution)/shard_map/while/body/eval_jaxpr/sub | solution.py:93
  13.5 5.3 %copy.18 = f32[1024,1024]{0,1:T(8,128)} copy(f32[1024,1024]{1,0:T(8,128)} %broadcast_bitcast_fusion.2) | data formatting | bytes 8388608 | tf_op jit(solution)/shard_map/while/body/eval_jaxpr/sub | solution.py:93
  18.8 6.0 %fusion.27 = f32[1024]{0:T(1024)S(1)} fusion(f32[1024,1024]{0,1:T(8,128)} %copy.18, f32[1024]{0:T(1024)S(1)} %bitcast.43, f32[1024]{0:T(1024)S(1)} %bitcast.44, bf16[1024,1024]{1,0:T(8,128)(2,1)S(1)} %get-tuple-element.270, bf16[1024,6144]{1,0:T(8,128)(2,1)} %get-tuple-element.269, s32[]{:T(128)S(6)} %select_n.12), kind=kOutput, calls=%fused_computation.1.clone.1 | convolution fusion | flops 2153774080 | bytes 8400900 | tf_op jit(solution)/shard_map/while/body/eval_jaxpr/dot_general | solution.py:91
  24.8 0.1 reduce_sum.73
  24.9 0.7 constant_dynamic-slice_fusion.3
  25.6 1.0 dynamic-slice_convert_fusion.2
  26.6 2.5 %broadcast_bitcast_fusion.2 = f32[1024,1024]{1,0:T(8,128)} fusion(f32[128,1024]{1,0:T(8,128)S(1)} %dynamic-slice_convert_fusion.2), kind=kLoop, calls=%fused_computation.6.clone.1 | loop fusion | bytes 4718592 | tf_op jit(solution)/shard_map/while/body/eval_jaxpr/sub | solution.py:93
  29.1 5.3 %copy.18 = f32[1024,1024]{0,1:T(8,128)} copy(f32[1024,1024]{1,0:T(8,128)} %broadcast_bitcast_fusion.2) | data formatting | bytes 8388608 | tf_op jit(solution)/shard_map/while/body/eval_jaxpr/sub | solution.py:93
  34.4 6.0 %fusion.27 = f32[1024]{0:T(1024)S(1)} fusion(f32[1024,1024]{0,1:T(8,128)} %copy.18, f32[1024]{0:T(1024)S(1)} %bitcast.43, f32[1024]{0:T(1024)S(1)} %bitcast.44, bf16[1024,1024]{1,0:T(8,128)(2,1)S(1)} %get-tuple-element.270, bf16[1024,6144]{1,0:T(8,128)(2,1)} %get-tuple-element.269, s32[]{:T(128)S(6)} %select_n.12), kind=kOutput, calls=%fused_computation.1.clone.1 | convolution fusion | flops 2153774080 | bytes 8400900 | tf_op jit(solution)/shard_map/while/body/eval_jaxpr/dot_general | solution.py:91
  40.4 0.1 reduce_sum.73
  40.5 0.7 constant_dynamic-slice_fusion.3
  41.2 1.0 dynamic-slice_convert_fusion.2
  42.2 2.5 %broadcast_bitcast_fusion.2 = f32[1024,1024]{1,0:T(8,128)} fusion(f32[128,1024]{1,0:T(8,128)S(1)} %dynamic-slice_convert_fusion.2), kind=kLoop, calls=%fused_computation.6.clone.1 | loop fusion | bytes 4718592 | tf_op jit(solution)/shard_map/while/body/eval_jaxpr/sub | solution.py:93
  44.7 5.3 %copy.18 = f32[1024,1024]{0,1:T(8,128)} copy(f32[1024,1024]{1,0:T(8,128)} %broadcast_bitcast_fusion.2) | data formatting | bytes 8388608 | tf_op jit(solution)/shard_map/while/body/eval_jaxpr/sub | solution.py:93
  50.0 6.0 %fusion.27 = f32[1024]{0:T(1024)S(1)} fusion(f32[1024,1024]{0,1:T(8,128)} %copy.18, f32[1024]{0:T(1024)S(1)} %bitcast.43, f32[1024]{0:T(1024)S(1)} %bitcast.44, bf16[1024,1024]{1,0:T(8,128)(2,1)S(1)} %get-tuple-element.270, bf16[1024,6144]{1,0:T(8,128)(2,1)} %get-tuple-element.269, s32[]{:T(128)S(6)} %select_n.12), kind=kOutput, calls=%fused_computation.1.clone.1 | convolution fusion | flops 2153774080 | bytes 8400900 | tf_op jit(solution)/shard_map/while/body/eval_jaxpr/dot_general | solution.py:91
  56.0 0.1 reduce_sum.73
  56.1 0.7 constant_dynamic-slice_fusion.3
  56.8 1.0 dynamic-slice_convert_fusion.2
  57.8 2.5 %broadcast_bitcast_fusion.2 = f32[1024,1024]{1,0:T(8,128)} fusion(f32[128,1024]{1,0:T(8,128)S(1)} %dynamic-slice_convert_fusion.2), kind=kLoop, calls=%fused_computation.6.clone.1 | loop fusion | bytes 4718592 | tf_op jit(solution)/shard_map/while/body/eval_jaxpr/sub | solution.py:93
  60.2 5.3 %copy.18 = f32[1024,1024]{0,1:T(8,128)} copy(f32[1024,1024]{1,0:T(8,128)} %broadcast_bitcast_fusion.2) | data formatting | bytes 8388608 | tf_op jit(solution)/shard_map/while/body/eval_jaxpr/sub | solution.py:93
  65.6 6.0 %fusion.27 = f32[1024]{0:T(1024)S(1)} fusion(f32[1024,1024]{0,1:T(8,128)} %copy.18, f32[1024]{0:T(1024)S(1)} %bitcast.43, f32[1024]{0:T(1024)S(1)} %bitcast.44, bf16[1024,1024]{1,0:T(8,128)(2,1)S(1)} %get-tuple-element.270, bf16[1024,6144]{1,0:T(8,128)(2,1)} %get-tuple-element.269, s32[]{:T(128)S(6)} %select_n.12), kind=kOutput, calls=%fused_computation.1.clone.1 | convolution fusion | flops 2153774080 | bytes 8400900 | tf_op jit(solution)/shard_map/while/body/eval_jaxpr/dot_general | solution.py:91
  71.5 0.1 reduce_sum.73
  71.7 0.7 constant_dynamic-slice_fusion.3
  72.4 1.0 dynamic-slice_convert_fusion.2
  73.4 2.5 %broadcast_bitcast_fusion.2 = f32[1024,1024]{1,0:T(8,128)} fusion(f32[128,1024]{1,0:T(8,128)S(1)} %dynamic-slice_convert_fusion.2), kind=kLoop, calls=%fused_computation.6.clone.1 | loop fusion | bytes 4718592 | tf_op jit(solution)/shard_map/while/body/eval_jaxpr/sub | solution.py:93
  75.8 5.3 %copy.18 = f32[1024,1024]{0,1:T(8,128)} copy(f32[1024,1024]{1,0:T(8,128)} %broadcast_bitcast_fusion.2) | data formatting | bytes 8388608 | tf_op jit(solution)/shard_map/while/body/eval_jaxpr/sub | solution.py:93
  81.2 6.0 %fusion.27 = f32[1024]{0:T(1024)S(1)} fusion(f32[1024,1024]{0,1:T(8,128)} %copy.18, f32[1024]{0:T(1024)S(1)} %bitcast.43, f32[1024]{0:T(1024)S(1)} %bitcast.44, bf16[1024,1024]{1,0:T(8,128)(2,1)S(1)} %get-tuple-element.270, bf16[1024,6144]{1,0:T(8,128)(2,1)} %get-tuple-element.269, s32[]{:T(128)S(6)} %select_n.12), kind=kOutput, calls=%fused_computation.1.clone.1 | convolution fusion | flops 2153774080 | bytes 8400900 | tf_op jit(solution)/shard_map/while/body/eval_jaxpr/dot_general | solution.py:91
  87.1 0.1 reduce_sum.73
  87.3 0.7 constant_dynamic-slice_fusion.3
  88.0 1.0 dynamic-slice_convert_fusion.2
  89.0 2.5 %broadcast_bitcast_fusion.2 = f32[1024,1024]{1,0:T(8,128)} fusion(f32[128,1024]{1,0:T(8,128)S(1)} %dynamic-slice_convert_fusion.2), kind=kLoop, calls=%fused_computation.6.clone.1 | loop fusion | bytes 4718592 | tf_op jit(solution)/shard_map/while/body/eval_jaxpr/sub | solution.py:93
  91.4 5.3 %copy.18 = f32[1024,1024]{0,1:T(8,128)} copy(f32[1024,1024]{1,0:T(8,128)} %broadcast_bitcast_fusion.2) | data formatting | bytes 8388608 | tf_op jit(solution)/shard_map/while/body/eval_jaxpr/sub | solution.py:93
  96.8 6.0 %fusion.27 = f32[1024]{0:T(1024)S(1)} fusion(f32[1024,1024]{0,1:T(8,128)} %copy.18, f32[1024]{0:T(1024)S(1)} %bitcast.43, f32[1024]{0:T(1024)S(1)} %bitcast.44, bf16[1024,1024]{1,0:T(8,128)(2,1)S(1)} %get-tuple-element.270, bf16[1024,6144]{1,0:T(8,128)(2,1)} %get-tuple-element.269, s32[]{:T(128)S(6)} %select_n.12), kind=kOutput, calls=%fused_computation.1.clone.1 | convolution fusion | flops 2153774080 | bytes 8400900 | tf_op jit(solution)/shard_map/while/body/eval_jaxpr/dot_general | solution.py:91
  102.7 0.1 reduce_sum.73
  103.5 1.9 %all-gather = f32[256,8]{1,0:T(8,128)S(1)} all-gather(f32[128,8]{1,0:T(8,128)S(1)} %broadcast_add_fusion), channel_id=2, replica_groups=mesh['samp'=64,'tp'=2] {'tp'}, dimensions={0}, use_global_device_ids=true | all-gather | bytes 12288 | tf_op jit(solution)/shard_map/all_gather | solution.py:21
  105.4 0.1 fusion.18
  105.5 0.2 exponential_reduce_fusion
  105.8 19.6 %all_to_all.5 = f32[64,2,128]{2,1,0:T(2,128)S(1)} all-to-all(f32[64,2,128]{2,1,0:T(2,128)S(1)} %broadcast_in_dim.11), channel_id=1, replica_groups=mesh['samp'=64,'tp'=2] {'samp'}, dimensions={0} | all-to-all | bytes 131072 | tf_op jit(solution)/shard_map/all_to_all | solution.py:26
  125.4 0.1 fusion.19
  125.9 0.5 add_multiply_fusion
  126.4 0.1 subtract_add_fusion
  126.5 0.7 copy.15
  (37 shorter events, 0.5 us)
Async XLA Ops:
  0.6 8.1 %copy-start = (f32[1,6144]{1,0:T(1,128)S(1)}, f32[1,6144]{1,0:T(1,128)}, u32[]{:S(2)}) copy-start(f32[1,6144]{1,0:T(1,128)} %param.19) | copy-start | bytes 73732
where the time goes:
time: 129 us; the launch traced here: 127 us
  local copies, waits for them, and re-layouts  53.3 us (41%)
  matrix products  37.5 us (29%)
  blocking collectives  24.5 us (19%)
  other arithmetic  10.1 us (8%)
  between operations  1.45 us (1%)
    sub x12, local copies, waits for them, and re-layouts, add_piece(): image_piece[:, None, :].astype(jnp.float32) - pixel_mean  46.8 us
    dot_general x6, matrix products, add_piece(): jnp.dot(hidden, w_piece, preferred_element_type=jnp.float32) + bias_piece  35.7 us
    all_to_all x1, blocking collectives, from_everyone(): lax.all_to_all(jnp.broadcast_to(shard[None], (length, *shard.shape)), axi...  19.6 us
    convert_element_type x6, other arithmetic, add_piece(): image_piece[:, None, :].astype(jnp.float32) - pixel_mean  5.94 us
    dynamic_slice x6, local copies, waits for them, and re-layouts, add_piece(): inverse_piece = lax.dynamic_slice_in_dim(inverse, offset, piece_width, 1)  4.16 us
    all_gather x1, blocking collectives, side_by_side(): lax.all_gather(both, axis, axis=dim, tiled=True)  3.02 us

commit v1 on v0

v1 whole, which is shorter than its diff:
```python
import functools
import math

import jax
import jax.numpy as jnp
from jax import lax
from jax.experimental import pallas as pl
from jax.experimental.pallas import tpu as pltpu
from jax.sharding import PartitionSpec as P

HALF_LOG_TAU = 0.9189385332046727
MESH = pl.DeviceIdType.MESH
F32 = jnp.float32
BF16 = jnp.bfloat16
NT = (((1,), (1,)), ((), ()))
G_ROWS = ((0, 48), (48, 48), (96, 48), (144, 48), (192, 32), (224, 32))
C_ROWS = ((0, 88), (88, 88), (176, 88), (264, 88), (352, 80), (432, 80))
SIDE = 4


def kernel(
    images, enc_mean, enc_ls, noise, w_in, b_in, w_out, b_out, pls,
    bound_ref, lw_ref,
    wv, ws, img, dv, bv, pv, nz, em, el, wbuf, bbuf, wat, lat, hid, gbuf, cbuf,
    s2v, acc_sq, pp, lsend, lrecv, sbuf, rbuf,
    in_sem, g_send, g_recv, pair_send, pair_recv, x_send, x_recv,
):
    me = lax.axis_index("samp")
    t = lax.axis_index("tp")
    x, y, z = me // (SIDE * SIDE), (me // SIDE) % SIDE, me % SIDE
    color = (x + y + z) % 2
    pixels = img.shape[1]
    all_pixels = 2 * pixels
    all_samples = 8 * SIDE * SIDE * SIDE

    def at(xx, yy, zz):
        return (xx % SIDE) * (SIDE * SIDE) + (yy % SIDE) * SIDE + zz % SIDE

    line = {
        "z": [at(x, y, z + k) for k in (1, 2, 3)],
        "y": [at(x, y + k, z) for k in (1, 2, 3)],
        "x": [at(x + k, y, z) for k in (1, 2, 3)],
    }
    near = [
        at(x + 1, y, z), at(x + 3, y, z), at(x, y + 1, z),
        at(x, y + 3, z), at(x, y, z + 1), at(x, y, z + 3),
    ]

    barrier = pltpu.get_barrier_semaphore()
    pl.semaphore_signal(barrier, inc=1, device_id=(me, 1 - t), device_id_type=MESH)
    for axis in ("x", "y", "z"):
        for other in line[axis]:
            pl.semaphore_signal(barrier, inc=1, device_id=(other, t), device_id_type=MESH)

    def slabs(p):
        return 2 * p, 2 * p + 1, 2 - p, 3 - 3 * p

    own = slabs(color)
    height = wv.shape[1]

    def load(src, dst, k):
        return pltpu.make_async_copy(src, dst, in_sem.at[k])

    loads = [
        load(noise, nz, 0), load(enc_mean, em, 1), load(enc_ls, el, 2),
        load(w_in, wbuf.at[t], 3), load(b_in, bbuf.at[t], 4),
        load(pls, pv, 5), load(b_out, bv, 6),
    ]
    slab = [
        load(w_out.at[pl.ds(pl.multiple_of(own[k] * height, height), height), :], wv.at[k], 7 + k)
        for k in range(4)
    ]
    load_img = load(images, img, 11)
    for c in loads:
        c.start()
    slab[0].start()
    load_img.start()
    for k in (1, 2, 3):
        slab[k].start()

    for k in (0, 1, 2):
        loads[k].wait()
    mean_t = em[...].T
    ls_t = el[...].T
    exp_t = jnp.exp(ls_t)
    ls_sum = jnp.sum(ls_t, axis=0, keepdims=True)
    for s in range(8):
        n_t = nz[pl.ds(s, 128, stride=8), :].T
        l_t = mean_t + exp_t * n_t
        lat[0:128, s * 128 : (s + 1) * 128] = l_t.astype(BF16)
        pp[s : s + 1, :] = 0.5 * jnp.sum(n_t * n_t - l_t * l_t, axis=0, keepdims=True) + ls_sum
    first_row = lax.broadcasted_iota(jnp.int32, (128, 1024), 0) == 0
    lat[128:256, :] = jnp.where(first_row, 1.0, 0.0).astype(BF16)

    loads[5].wait()
    loads[6].wait()
    s2v[...] = jnp.exp(-2.0 * pv[...])
    total_ls = jnp.sum(pv[...], axis=1, keepdims=True)

    def scale(k):
        for c in range(pixels // 256):
            cols = slice(c * 256, (c + 1) * 256)
            factor = s2v[:, cols].astype(BF16)
            ws[k, :, cols] = wv[k, :, cols] * factor

    def gram(k, j):
        return lax.dot_general(ws[k], wv[j], NT, preferred_element_type=F32)

    def sends(q):
        out = []
        for d in range(6):
            lo, n = G_ROWS[d] if q < 5 else C_ROWS[d]
            ref = gbuf.at[color, q, pl.ds(lo, n), :] if q < 5 else cbuf.at[color, pl.ds(lo, n), :]
            out.append(
                pltpu.make_async_remote_copy(
                    src_ref=ref, dst_ref=ref, send_sem=g_send.at[q, d], recv_sem=g_recv.at[q, d],
                    device_id=(near[d], t), device_id_type=MESH,
                )
            )
        return out

    def receives(q):
        out = []
        for d in range(6):
            lo, n = G_ROWS[d] if q < 5 else C_ROWS[d]
            c = 1 - color
            ref = gbuf.at[c, q, pl.ds(lo, n), :] if q < 5 else cbuf.at[c, pl.ds(lo, n), :]
            out.append(
                pltpu.make_async_remote_copy(
                    src_ref=ref, dst_ref=ref, send_sem=g_send.at[q, d], recv_sem=g_recv.at[q, d],
                    device_id=(near[d], t), device_id_type=MESH,
                )
            )
        return out

    all_sends = [sends(q) for q in range(6)]

    slab[0].wait()
    scale(0)
    load_img.wait()
    acc_sq[...] = jnp.zeros_like(acc_sq)
    gbuf[color, 0] = (0.5 * gram(0, 0)).astype(BF16)
    for c in range(pixels // 256):
        cols = slice(c * 256, (c + 1) * 256)
        d = img[:, cols].astype(F32) - bv[:, cols]
        e = d * s2v[:, cols]
        hi = e.astype(BF16)
        dv[0:128, cols] = hi
        dv[128:256, cols] = (e - hi.astype(F32)).astype(BF16)
        sq = d * e
        acc_sq[...] += sq[:, 0:128] + sq[:, 128:256]

    loads[3].wait()
    loads[4].wait()
    pl.semaphore_wait(barrier, 10)
    weights = pltpu.make_async_remote_copy(
        src_ref=wbuf.at[t], dst_ref=wbuf.at[t], send_sem=pair_send.at[0], recv_sem=pair_recv.at[0],
        device_id=(me, 1 - t), device_id_type=MESH,
    )
    biases = pltpu.make_async_remote_copy(
        src_ref=bbuf.at[t], dst_ref=bbuf.at[t], send_sem=pair_send.at[1], recv_sem=pair_recv.at[1],
        device_id=(me, 1 - t), device_id_type=MESH,
    )
    weights.start()
    biases.start()
    for c in all_sends[0]:
        c.start()

    slab[1].wait()
    scale(1)
    gbuf[color, 1] = gram(0, 1).astype(BF16)
    for c in all_sends[1]:
        c.start()
    gbuf[color, 2] = (0.5 * gram(1, 1)).astype(BF16)
    for c in all_sends[2]:
        c.start()
    for k in range(2):
        both = lax.dot_general(wv[k], dv[...], NT, preferred_element_type=F32)
        cbuf[color, k * 256 : (k + 1) * 256, :] = both[:, 0:128] + both[:, 128:256]
    for c in all_sends[5]:
        c.start()
    slab[2].wait()
    gbuf[color, 3] = gram(0, 2).astype(BF16)
    for c in all_sends[3]:
        c.start()
    slab[3].wait()
    gbuf[color, 4] = gram(1, 3).astype(BF16)
    for c in all_sends[4]:
        c.start()

    theirs_w = pltpu.make_async_remote_copy(
        src_ref=wbuf.at[1 - t], dst_ref=wbuf.at[1 - t], send_sem=pair_send.at[0], recv_sem=pair_recv.at[0],
        device_id=(me, 1 - t), device_id_type=MESH,
    )
    theirs_b = pltpu.make_async_remote_copy(
        src_ref=bbuf.at[1 - t], dst_ref=bbuf.at[1 - t], send_sem=pair_send.at[1], recv_sem=pair_recv.at[1],
        device_id=(me, 1 - t), device_id_type=MESH,
    )
    theirs_w.wait_recv()
    theirs_b.wait_recv()
    for k in range(2):
        row0 = lax.broadcasted_iota(jnp.int32, (128, 512), 0) == 0
        bias = jnp.where(row0, bbuf[k].astype(F32), 0.0)
        wat[k * 512 : (k + 1) * 512, 0:128] = wbuf[k].astype(F32).T.astype(BF16)
        wat[k * 512 : (k + 1) * 512, 128:256] = bias.T.astype(BF16)
    for k in range(4):
        rows = slice(k * 256, (k + 1) * 256)
        pre = jnp.dot(wat[rows, :], lat[...], preferred_element_type=F32)
        hid[k] = jnp.maximum(pre, 0.0).astype(BF16)

    def apply(p, which):
        o1, o2, x1, x2 = slabs(p)
        for n in range(4):
            cols = slice(n * 256, (n + 1) * 256)
            y1 = jnp.dot(gbuf[p, 0], hid[o1, :, cols], preferred_element_type=F32)
            y1 += jnp.dot(gbuf[p, 1], hid[o2, :, cols], preferred_element_type=F32)
            y1 += jnp.dot(gbuf[p, 3], hid[x1, :, cols], preferred_element_type=F32)
            y2 = jnp.dot(gbuf[p, 2], hid[o2, :, cols], preferred_element_type=F32)
            y2 += jnp.dot(gbuf[p, 4], hid[x2, :, cols], preferred_element_type=F32)
            for h in range(2):
                s = 2 * n + h
                part = slice(h * 128, (h + 1) * 128)
                lanes = slice(s * 128, (s + 1) * 128)
                total = jnp.sum(
                    (cbuf[p, 0:256, :] - y1[:, part]) * hid[o1, :, lanes].astype(F32)
                    + (cbuf[p, 256:512, :] - y2[:, part]) * hid[o2, :, lanes].astype(F32),
                    axis=0, keepdims=True,
                )
                if which == 0:
                    lsend[s : s + 1, :] = total
                else:
                    lsend[s : s + 1, :] += total

    apply(color, 0)
    image_part = -0.5 * jnp.sum(acc_sq[...].T, axis=0, keepdims=True)
    lsend[8:16, :] = jnp.broadcast_to(image_part - total_ls - pixels * HALF_LOG_TAU, (8, 128))
    for q in (0, 1, 2, 5, 3, 4):
        for c in receives(q):
            c.wait_recv()
    apply(1 - color, 1)

    share = pltpu.make_async_remote_copy(
        src_ref=lsend, dst_ref=lrecv, send_sem=pair_send.at[2], recv_sem=pair_recv.at[2],
        device_id=(me, 1 - t), device_id_type=MESH,
    )
    share.start()
    share.wait_recv()
    loglik = lsend[...] + lrecv[...]
    image_term = loglik[8:9, :]
    logw = loglik[0:8, :] + pp[...]
    peak = jnp.max(logw, axis=0, keepdims=True)
    sums = jnp.sum(jnp.exp(logw - peak), axis=0, keepdims=True)
    rounds = []
    for r, axis in enumerate(("z", "y", "x")):
        sbuf[r, 0:1, :] = peak
        sbuf[r, 1:2, :] = sums
        copies = [
            pltpu.make_async_remote_copy(
                src_ref=sbuf.at[r], dst_ref=rbuf.at[r, k], send_sem=x_send.at[r, k],
                recv_sem=x_recv.at[r, k], device_id=(line[axis][k], t), device_id_type=MESH,
            )
            for k in range(3)
        ]
        for c in copies:
            c.start()
        for c in copies:
            c.wait_recv()
        rounds += copies
        top = peak
        for k in range(3):
            top = jnp.maximum(top, rbuf[r, k, 0:1, :])
        sums = sums * jnp.exp(peak - top)
        for k in range(3):
            sums += rbuf[r, k, 1:2, :] * jnp.exp(rbuf[r, k, 0:1, :] - top)
        peak = top
    log_sum = jnp.log(sums)
    log_all = math.log(all_samples)
    bound_ref[...] = (image_term + peak + log_sum - log_all) / all_pixels
    lw_ref[...] = logw - peak - log_sum + log_all

    for c in rounds + [share, weights, biases]:
        c.wait_send()
    for q in range(6):
        for c in all_sends[q]:
            c.wait_send()


def on_device(images, enc_mean, enc_logscale, noise, w_in, b_in, w_out, b_out, pixel_logscale):
    image_count, sample_count, latent_dims = noise.shape
    hidden, pixels = w_out.shape
    height = hidden // 4
    noise = noise.reshape(image_count * sample_count, latent_dims)
    half = w_in.shape[1]
    V = pltpu.VMEM
    bound, lw = pl.pallas_call(
        kernel,
        out_shape=(
            jax.ShapeDtypeStruct((1, image_count), F32),
            jax.ShapeDtypeStruct((sample_count, image_count), F32),
        ),
        in_specs=[pl.BlockSpec(memory_space=pl.ANY)] * 9,
        out_specs=[pl.BlockSpec(memory_space=pltpu.VMEM)] * 2,
        scratch_shapes=[
            V((4, height, pixels), BF16), V((2, height, pixels), BF16), V((image_count, pixels), BF16),
            V((2 * image_count, pixels), BF16), V((1, pixels), F32), V((1, pixels), F32),
            V(noise.shape, F32), V((image_count, latent_dims), F32), V((image_count, latent_dims), F32),
            V((2, latent_dims, half), BF16), V((2, 1, half), BF16), V((hidden, 256), BF16),
            V((256, image_count * sample_count), BF16), V((4, height, image_count * sample_count), BF16),
            V((2, 5, height, height), BF16), V((2, 2 * height, image_count), F32),
            V((1, pixels), F32), V((image_count, 128), F32), V((sample_count, image_count), F32),
            V((16, image_count), F32), V((16, image_count), F32),
            V((3, 8, image_count), F32), V((3, 3, 8, image_count), F32),
            pltpu.SemaphoreType.DMA((12,)), pltpu.SemaphoreType.DMA((6, 6)), pltpu.SemaphoreType.DMA((6, 6)),
            pltpu.SemaphoreType.DMA((3,)), pltpu.SemaphoreType.DMA((3,)),
            pltpu.SemaphoreType.DMA((3, 3)), pltpu.SemaphoreType.DMA((3, 3)),
        ],
        compiler_params=pltpu.CompilerParams(
            collective_id=0, has_side_effects=True, vmem_limit_bytes=60 * 1024 * 1024
        ),
    )(images, enc_mean, enc_logscale, noise, w_in, b_in, w_out, b_out, pixel_logscale)
    return bound.reshape(image_count), lw.T


def solution(mesh):
    pixel_split = P(None, "tp")
    in_specs = (
        pixel_split, P(), P(), P(None, "samp", None),
        pixel_split, pixel_split, pixel_split, pixel_split, pixel_split,
    )
    out_specs = (P(), P(None, "samp"))
    return jax.shard_map(
        on_device, mesh=mesh, in_specs=in_specs, out_specs=out_specs, check_vma=False
    )
```

time: 129 us -> 39.1 us (0.30)
  local copies, waits for them, and re-layouts: 53.3 us -> 2.4 us
  matrix products: 37.5 us -> 0 us
  Pallas kernels: 0 us -> 35.3 us
  blocking collectives: 24.5 us -> 0 us
  other arithmetic: 10.1 us -> 0 us
    sub x12 -> x0, local copies, waits for them, and re-layouts: 46.8 us -> none  [add_piece(): image_piece[:, None, :].astype(jnp.float32) - pixel_mean]
    dot_general x7 -> x0, matrix products: 37.5 us -> none  [the longest x6 35.7 us: add_piece(): jnp.dot(hidden, w_piece, preferred_element_type=jnp.float32) + bias_piece]
    pallas_call x0 -> x1, Pallas kernels: none -> 35.3 us  [on_device(): pl.pallas_call(kernel, out_shape=(jax.ShapeDtypeStruct((1, image_count),...]
    all_to_all x1 -> x0, blocking collectives: 19.6 us -> none  [from_everyone(): lax.all_to_all(jnp.broadcast_to(shard[None], (length, *shard.shape)), axi...]
    convert_element_type x6 -> x0, other arithmetic: 5.94 us -> none  [add_piece(): image_piece[:, None, :].astype(jnp.float32) - pixel_mean]
    all_gather x2 -> x0, blocking collectives: 4.93 us -> none  [the longest x1 3.02 us: side_by_side(): lax.all_gather(both, axis, axis=dim, tiled=True)]
    dynamic_slice x6 -> x0, local copies, waits for them, and re-layouts: 4.16 us -> none  [add_piece(): inverse_piece = lax.dynamic_slice_in_dim(inverse, offset, piece_width, 1)]
    reduce_sum x4 -> x0, other arithmetic: 2.31 us -> none  [the longest x1 1.45 us: on_device(): prior = jnp.sum(-0.5 * latent * latent - HALF_LOG_TAU, axis=2)]
where the time goes in v1:
time: 39.1 us; the launch traced here: 38.3 us
  Pallas kernels  35.3 us (90%)
  local copies, waits for them, and re-layouts  2.4 us (6%)
  between operations  0.64 us (2%)
    pallas_call x1, Pallas kernels, on_device(): pl.pallas_call(kernel, out_shape=(jax.ShapeDtypeStruct((1, image_count),...  35.3 us
    unnamed x2, local copies, waits for them, and re-layouts  2.4 us

profile of v1, /device:TPU:1, one launch (start us, length us, event | category | flops | bytes accessed | tf_op | source)
XLA Modules:
  0.0 38.3 jit_solution(8097898092537724809)
XLA Ops:
  0.6 35.3 %shard_map.104 = (f32[1,128]{1,0:T(1,128)}, f32[8,128]{1,0:T(8,128)}) custom-call(bf16[128,6144]{1,0:T(8,128)(2,1)} %images.1, f32[128,128]{1,0:T(8,128)} %enc_mean.1, f32[128,128]{1,0:T(8,128)} %enc_ls.1, f32[1024,128]{1,0:T(8,128)} %bitcast.3, bf16[128,512]{1,0:T(8,128)(2,1)} %w_in.1, bf16[1,512]{1,0:T(2,128)(2,1)} %b_in.1, bf16[1024,6144]{1,0:T(8,128)(2,1)} %w_out.1, ...), custom_call_target="tpu_custom_call" | custom-call | tf_op jit(solution)/shard_map/pallas_call | solution.py:295
  35.9 1.1 %copy.13 = f32[128]{0:T(128)} copy(f32[128]{0:T(128)} %bitcast.5) | data formatting | bytes 1024
  37.1 1.3 %copy.14 = f32[128,8]{0,1:T(8,128)} copy(f32[128,8]{0,1:T(8,128)} %bitcast.4) | data formatting | bytes 8192

commit v2 on v1

v2 whole, which is shorter than its diff:
```python
import functools
import math

import jax
import jax.numpy as jnp
from jax import lax
from jax.experimental import pallas as pl
from jax.experimental.pallas import tpu as pltpu
from jax.sharding import PartitionSpec as P

HALF_LOG_TAU = 0.9189385332046727
MESH = pl.DeviceIdType.MESH
F32 = jnp.float32
BF16 = jnp.bfloat16
NT = (((1,), (1,)), ((), ()))
G_ROWS = ((0, 48), (48, 48), (96, 48), (144, 48), (192, 32), (224, 32))
C_ROWS = ((0, 88), (88, 88), (176, 88), (264, 88), (352, 80), (432, 80))
SIDE = 4


def kernel(
    images, enc_mean, enc_ls, noise, w_in, b_in, w_out, b_out, pls,
    bound_ref, lw_ref,
    wv, ws, img, dv, bv, pv, nz, em, el, wbuf, bbuf, wat, lat, hid, gbuf, cbuf,
    g_half, s2v, acc_sq, pp, lsend, lrecv, sbuf, rbuf,
    in_sem, g_send, g_recv, pair_send, pair_recv, x_send, x_recv,
):
    me = lax.axis_index("samp")
    t = lax.axis_index("tp")
    x, y, z = me // (SIDE * SIDE), (me // SIDE) % SIDE, me % SIDE
    color = (x + y + z) % 2
    pixels = img.shape[1]
    all_pixels = 2 * pixels
    all_samples = 8 * SIDE * SIDE * SIDE

    def at(xx, yy, zz):
        return (xx % SIDE) * (SIDE * SIDE) + (yy % SIDE) * SIDE + zz % SIDE

    line = {
        "z": [at(x, y, z + k) for k in (1, 2, 3)],
        "y": [at(x, y + k, z) for k in (1, 2, 3)],
        "x": [at(x + k, y, z) for k in (1, 2, 3)],
    }
    near = [
        at(x + 1, y, z), at(x + 3, y, z), at(x, y + 1, z),
        at(x, y + 3, z), at(x, y, z + 1), at(x, y, z + 3),
    ]

    barrier = pltpu.get_barrier_semaphore()
    pl.semaphore_signal(barrier, inc=1, device_id=(me, 1 - t), device_id_type=MESH)
    for axis in ("x", "y", "z"):
        for other in line[axis]:
            pl.semaphore_signal(barrier, inc=1, device_id=(other, t), device_id_type=MESH)

    def slabs(p):
        return 2 * p, 2 * p + 1, 2 - p, 3 - 3 * p

    own = slabs(color)
    height = wv.shape[1]
    step = 512
    chunks = pixels // step

    def load(src, dst, k):
        return pltpu.make_async_copy(src, dst, in_sem.at[k])

    def w_rows(k):
        return pl.ds(pl.multiple_of(own[k] * height, height), height)

    load_pls, load_b = load(pls, pv, 0), load(b_out, bv, 1)
    half = pixels // 2
    load_w0 = [
        load(w_out.at[w_rows(0), pl.ds(k * half, half)], wv.at[0, :, pl.ds(k * half, half)], 2 + k)
        for k in range(2)
    ]
    load_img = load(images, img, 4)
    load_w = [load(w_out.at[w_rows(k), :], wv.at[k], 4 + k) for k in (1, 2, 3)]
    load_in = [load(w_in, wbuf.at[t], 8), load(b_in, bbuf.at[t], 9)]
    load_lat = [load(noise, nz, 10), load(enc_mean, em, 11), load(enc_ls, el, 12)]
    for c in [load_pls, load_w0[0], load_w0[1], load_b, load_img, load_w[0]]:
        c.start()
    for c in load_in + load_lat + load_w[1:]:
        c.start()

    def piece(c):
        return slice(c * step, (c + 1) * step)

    def scale(k, c):
        for q in range(2):
            cols = slice(c * step + q * 256, c * step + (q + 1) * 256)
            ws[k, :, cols] = wv[k, :, cols] * s2v[:, cols].astype(BF16)

    def differences(c):
        for q in range(2):
            cols = slice(c * step + q * 256, c * step + (q + 1) * 256)
            d = img[:, cols].astype(F32) - bv[:, cols]
            e = d * s2v[:, cols]
            hi = e.astype(BF16)
            dv[0:128, cols] = hi
            dv[128:256, cols] = (e - hi.astype(F32)).astype(BF16)
            sq = d * e
            acc_sq[...] += sq[:, 0:128] + sq[:, 128:256]

    def nt(a, b):
        return lax.dot_general(a, b, NT, preferred_element_type=F32)

    def block(body):
        pl.when(t < 2)(body)

    def plus(total, more):
        return more if total is None else total + more

    def two_grams(first, second, beside):
        a = b = None
        for c in range(chunks):
            cols = piece(c)
            a = plus(a, nt(first[0][first[1], :, cols], first[2](cols)))
            b = plus(b, nt(second[0][second[1], :, cols], second[2](cols)))
            beside(c)
        return a, b

    def exchange(q):
        out = []
        for d in range(6):
            lo, n = G_ROWS[d] if q < 5 else C_ROWS[d]
            mine = gbuf.at[color, q, pl.ds(lo, n), :] if q < 5 else cbuf.at[color, pl.ds(lo, n), :]
            out.append(
                pltpu.make_async_remote_copy(
                    src_ref=mine, dst_ref=mine, send_sem=g_send.at[q, d], recv_sem=g_recv.at[q, d],
                    device_id=(near[d], t), device_id_type=MESH,
                )
            )
        return out

    def arrivals(q):
        out = []
        for d in range(6):
            lo, n = G_ROWS[d] if q < 5 else C_ROWS[d]
            c = 1 - color
            ref = gbuf.at[c, q, pl.ds(lo, n), :] if q < 5 else cbuf.at[c, pl.ds(lo, n), :]
            out.append(
                pltpu.make_async_remote_copy(
                    src_ref=ref, dst_ref=ref, send_sem=g_send.at[q, d], recv_sem=g_recv.at[q, d],
                    device_id=(near[d], t), device_id_type=MESH,
                )
            )
        return out

    all_sends = [exchange(q) for q in range(6)]

    def send(q):
        for c in all_sends[q]:
            c.start()

    load_pls.wait()
    s2v[...] = jnp.exp(-2.0 * pv[...])
    total_ls = jnp.sum(pv[...], axis=1, keepdims=True)
    acc_sq[...] = jnp.zeros_like(acc_sq)
    load_w0[0].wait()
    def half_gram(k):
        def body():
            parts = [None, None]
            first, last = k * (chunks // 2), (k + 1) * (chunks // 2)
            scale(0, first)
            scale(0, first + 1)
            for c in range(first, last):
                parts[c % 2] = plus(parts[c % 2], nt(ws[0, :, piece(c)], wv[0, :, piece(c)]))
                if c + 2 < last:
                    scale(0, c + 2)
            both = parts[0] + parts[1]
            if k == 0:
                g_half[...] = both
            else:
                gbuf[color, 0] = (0.5 * (g_half[...] + both)).astype(BF16)

        block(body)

    half_gram(0)
    load_w0[1].wait()
    half_gram(1)
    for c in load_in:
        c.wait()
    pl.semaphore_wait(barrier, 10)

    def pair_copy(ref, k):
        return pltpu.make_async_remote_copy(
            src_ref=ref, dst_ref=ref, send_sem=pair_send.at[k], recv_sem=pair_recv.at[k],
            device_id=(me, 1 - t), device_id_type=MESH,
        )

    weights, biases = pair_copy(wbuf.at[t], 0), pair_copy(bbuf.at[t], 1)
    weights.start()
    biases.start()
    send(0)
    load_b.wait()
    load_img.wait()
    load_w[0].wait()
    def beside_gram(c):
        if c + 1 < chunks:
            scale(1, c + 1)
        differences(c)

    rhs1 = lambda cols: wv[1, :, cols]

    @block
    def _():
        scale(1, 0)
        g1, g2 = two_grams((ws, 0, rhs1), (ws, 1, rhs1), beside_gram)
        gbuf[color, 1] = g1.astype(BF16)
        gbuf[color, 2] = (0.5 * g2).astype(BF16)

    send(1)
    send(2)
    for c in load_lat:
        c.wait()
    rhs_d = lambda cols: dv[:, cols]

    @block
    def _():
        mean_t = em[...].T
        ls_t = el[...].T
        exp_t = jnp.exp(ls_t)
        ls_sum = jnp.sum(ls_t, axis=0, keepdims=True)
        first_row = lax.broadcasted_iota(jnp.int32, (128, 1024), 0) == 0
        lat[128:256, :] = jnp.where(first_row, 1.0, 0.0).astype(BF16)

        def beside_cross(c):
            if c < 8:
                n_t = nz[pl.ds(c, 128, stride=8), :].T
                l_t = mean_t + exp_t * n_t
                lat[0:128, c * 128 : (c + 1) * 128] = l_t.astype(BF16)
                squares = jnp.sum(n_t * n_t - l_t * l_t, axis=0, keepdims=True)
                pp[c : c + 1, :] = 0.5 * squares + ls_sum

        c1, c2 = two_grams((wv, 0, rhs_d), (wv, 1, rhs_d), beside_cross)
        cbuf[color, 0:256, :] = c1[:, 0:128] + c1[:, 128:256]
        cbuf[color, 256:512, :] = c2[:, 0:128] + c2[:, 128:256]

    send(5)
    pair_copy(wbuf.at[1 - t], 0).wait_recv()
    pair_copy(bbuf.at[1 - t], 1).wait_recv()
    load_w[1].wait()
    load_w[2].wait()
    row0 = lax.broadcasted_iota(jnp.int32, (128, 128), 0) == 0

    def beside_last(c):
        if c < 8:
            k, lo = c // 4, (c % 4) * 128
            rows = slice(c * 128, (c + 1) * 128)
            wat[rows, 0:128] = wbuf[k, :, lo : lo + 128].astype(F32).T.astype(BF16)
            bias = jnp.where(row0, bbuf[k, :, lo : lo + 128].astype(F32), 0.0)
            wat[rows, 128:256] = bias.T.astype(BF16)

    rhs2, rhs3 = (lambda cols: wv[2, :, cols]), (lambda cols: wv[3, :, cols])

    @block
    def _():
        g3, g4 = two_grams((ws, 0, rhs2), (ws, 1, rhs3), beside_last)
        gbuf[color, 3] = g3.astype(BF16)
        gbuf[color, 4] = g4.astype(BF16)

    send(3)
    send(4)
    @block
    def _():
        for k in range(4):
            rows = slice(k * 256, (k + 1) * 256)
            pre = jnp.dot(wat[rows, :], lat[...], preferred_element_type=F32)
            hid[k] = jnp.maximum(pre, 0.0).astype(BF16)


    def apply(p, which):
        o1, o2, x1, x2 = slabs(p)
        for n in range(4):
            cols = slice(n * 256, (n + 1) * 256)

            def long():
                y = jnp.dot(gbuf[p, 0], hid[o1, :, cols], preferred_element_type=F32)
                y += jnp.dot(gbuf[p, 1], hid[o2, :, cols], preferred_element_type=F32)
                return y + jnp.dot(gbuf[p, 3], hid[x1, :, cols], preferred_element_type=F32)

            def short():
                y = jnp.dot(gbuf[p, 2], hid[o2, :, cols], preferred_element_type=F32)
                return y + jnp.dot(gbuf[p, 4], hid[x2, :, cols], preferred_element_type=F32)

            if n % 2 == 0:
                y1 = long()
                y2 = short()
            else:
                y2 = short()
                y1 = long()
            for h in range(2):
                s = 2 * n + h
                part = slice(h * 128, (h + 1) * 128)
                lanes = slice(s * 128, (s + 1) * 128)
                total = jnp.sum(
                    (cbuf[p, 0:256, :] - y1[:, part]) * hid[o1, :, lanes].astype(F32)
                    + (cbuf[p, 256:512, :] - y2[:, part]) * hid[o2, :, lanes].astype(F32),
                    axis=0, keepdims=True,
                )
                if which == 0:
                    lsend[s : s + 1, :] = total
                else:
                    lsend[s : s + 1, :] += total

    block(functools.partial(apply, color, 0))
    image_part = -0.5 * jnp.sum(acc_sq[...].T, axis=0, keepdims=True)
    lsend[8:16, :] = jnp.broadcast_to(image_part - total_ls - pixels * HALF_LOG_TAU, (8, 128))
    for q in (0, 1, 2, 5, 3, 4):
        for c in arrivals(q):
            c.wait_recv()
    block(functools.partial(apply, 1 - color, 1))

    share = pltpu.make_async_remote_copy(
        src_ref=lsend, dst_ref=lrecv, send_sem=pair_send.at[2], recv_sem=pair_recv.at[2],
        device_id=(me, 1 - t), device_id_type=MESH,
    )
    share.start()
    share.wait_recv()
    loglik = lsend[...] + lrecv[...]
    image_term = loglik[8:9, :]
    logw = loglik[0:8, :] + pp[...]
    peak = jnp.max(logw, axis=0, keepdims=True)
    sums = jnp.sum(jnp.exp(logw - peak), axis=0, keepdims=True)
    rounds = []
    for r, axis in enumerate(("z", "y", "x")):
        sbuf[r, 0:1, :] = peak
        sbuf[r, 1:2, :] = sums
        copies = [
            pltpu.make_async_remote_copy(
                src_ref=sbuf.at[r], dst_ref=rbuf.at[r, k], send_sem=x_send.at[r, k],
                recv_sem=x_recv.at[r, k], device_id=(line[axis][k], t), device_id_type=MESH,
            )
            for k in range(3)
        ]
        for c in copies:
            c.start()
        for c in copies:
            c.wait_recv()
        rounds += copies
        top = peak
        for k in range(3):
            top = jnp.maximum(top, rbuf[r, k, 0:1, :])
        sums = sums * jnp.exp(peak - top)
        for k in range(3):
            sums += rbuf[r, k, 1:2, :] * jnp.exp(rbuf[r, k, 0:1, :] - top)
        peak = top
    log_sum = jnp.log(sums)
    log_all = math.log(all_samples)
    bound_ref[...] = (image_term + peak + log_sum - log_all) / all_pixels
    lw_ref[...] = logw - peak - log_sum + log_all

    for c in rounds + [share, weights, biases]:
        c.wait_send()
    for q in range(6):
        for c in all_sends[q]:
            c.wait_send()


def on_device(images, enc_mean, enc_logscale, noise, w_in, b_in, w_out, b_out, pixel_logscale):
    image_count, sample_count, latent_dims = noise.shape
    hidden, pixels = w_out.shape
    height = hidden // 4
    noise = noise.reshape(image_count * sample_count, latent_dims)
    half = w_in.shape[1]
    V = pltpu.VMEM
    bound, lw = pl.pallas_call(
        kernel,
        out_shape=(
            jax.ShapeDtypeStruct((1, image_count), F32),
            jax.ShapeDtypeStruct((sample_count, image_count), F32),
        ),
        in_specs=[pl.BlockSpec(memory_space=pl.ANY)] * 9,
        out_specs=[pl.BlockSpec(memory_space=pltpu.VMEM)] * 2,
        scratch_shapes=[
            V((4, height, pixels), BF16), V((2, height, pixels), BF16), V((image_count, pixels), BF16),
            V((2 * image_count, pixels), BF16), V((1, pixels), F32), V((1, pixels), F32),
            V(noise.shape, F32), V((image_count, latent_dims), F32), V((image_count, latent_dims), F32),
            V((2, latent_dims, half), BF16), V((2, 1, half), BF16), V((hidden, 256), BF16),
            V((256, image_count * sample_count), BF16), V((4, height, image_count * sample_count), BF16),
            V((2, 5, height, height), BF16), V((2, 2 * height, image_count), F32),
            V((height, height), F32), V((1, pixels), F32), V((image_count, 128), F32), V((sample_count, image_count), F32),
            V((16, image_count), F32), V((16, image_count), F32),
            V((3, 8, image_count), F32), V((3, 3, 8, image_count), F32),
            pltpu.SemaphoreType.DMA((13,)), pltpu.SemaphoreType.DMA((6, 6)), pltpu.SemaphoreType.DMA((6, 6)),
            pltpu.SemaphoreType.DMA((3,)), pltpu.SemaphoreType.DMA((3,)),
            pltpu.SemaphoreType.DMA((3, 3)), pltpu.SemaphoreType.DMA((3, 3)),
        ],
        compiler_params=pltpu.CompilerParams(
            collective_id=0, has_side_effects=True, vmem_limit_bytes=60 * 1024 * 1024
        ),
    )(images, enc_mean, enc_logscale, noise, w_in, b_in, w_out, b_out, pixel_logscale)
    return bound.reshape(image_count), lw.T


def solution(mesh):
    pixel_split = P(None, "tp")
    in_specs = (
        pixel_split, P(), P(), P(None, "samp", None),
        pixel_split, pixel_split, pixel_split, pixel_split, pixel_split,
    )
    out_specs = (P(), P(None, "samp"))
    return jax.shard_map(
        on_device, mesh=mesh, in_specs=in_specs, out_specs=out_specs, check_vma=False
    )
```

time: 39.1 us -> 34.5 us (0.88)
  the two profiles are of different devices: /device:TPU:1 before, /device:TPU:0 now
where the time goes in v2:
time: 34.5 us; the launch traced here: 34.3 us
  Pallas kernels  31.3 us (91%)
  local copies, waits for them, and re-layouts  2.4 us (7%)
  between operations  0.64 us (2%)
    pallas_call x1, Pallas kernels, on_device(): pl.pallas_call(kernel, out_shape=(jax.ShapeDtypeStruct((1, image_count),...  31.3 us
    unnamed x2, local copies, waits for them, and re-layouts  2.4 us

profile of v2, /device:TPU:0, one launch (start us, length us, event | category | flops | bytes accessed | tf_op | source)
XLA Modules:
  0.0 34.3 jit_solution(4620210541717227680)
XLA Ops:
  0.6 31.3 %shard_map.104 = (f32[1,128]{1,0:T(1,128)}, f32[8,128]{1,0:T(8,128)}) custom-call(bf16[128,6144]{1,0:T(8,128)(2,1)} %images.1, f32[128,128]{1,0:T(8,128)} %enc_mean.1, f32[128,128]{1,0:T(8,128)} %enc_ls.1, f32[1024,128]{1,0:T(8,128)} %bitcast.3, bf16[128,512]{1,0:T(8,128)(2,1)} %w_in.1, bf16[1,512]{1,0:T(2,128)(2,1)} %b_in.1, bf16[1024,6144]{1,0:T(8,128)(2,1)} %w_out.1, ...), custom_call_target="tpu_custom_call" | custom-call | tf_op jit(solution)/shard_map/pallas_call | solution.py:366
  31.9 1.1 %copy.13 = f32[128]{0:T(128)} copy(f32[128]{0:T(128)} %bitcast.5) | data formatting | bytes 1024
  33.1 1.3 %copy.14 = f32[128,8]{0,1:T(8,128)} copy(f32[128,8]{0,1:T(8,128)} %bitcast.4) | data formatting | bytes 8192

commit v3 on v2

--- a/solution.py
+++ b/solution.py
@@ -14,16 +14,18 @@
 BF16 = jnp.bfloat16
 NT = (((1,), (1,)), ((), ()))
 G_ROWS = ((0, 48), (48, 48), (96, 48), (144, 48), (192, 32), (224, 32))
-C_ROWS = ((0, 88), (88, 88), (176, 88), (264, 88), (352, 80), (432, 80))
+C_ROWS = ((0, 48), (48, 48), (96, 40), (136, 40), (176, 40), (216, 40))
 SIDE = 4
+FINAL = pltpu.VMEM
 
 
 def kernel(
     images, enc_mean, enc_ls, noise, w_in, b_in, w_out, b_out, pls,
-    bound_ref, lw_ref,
+    out_ref,
     wv, ws, img, dv, bv, pv, nz, em, el, wbuf, bbuf, wat, lat, hid, gbuf, cbuf,
     g_half, s2v, acc_sq, pp, lsend, lrecv, sbuf, rbuf,
     in_sem, g_send, g_recv, pair_send, pair_recv, x_send, x_recv,
+    plane_sem, cube_sem,
 ):
     me = lax.axis_index("samp")
     t = lax.axis_index("tp")
@@ -45,6 +47,12 @@
         at(x + 1, y, z), at(x + 3, y, z), at(x, y + 1, z),
         at(x, y + 3, z), at(x, y, z + 1), at(x, y, z + 3),
     ]
+
+    far = [lax.rem(x + k, SIDE) * (SIDE * SIDE) for k in range(SIDE)]
+    mid = [lax.rem(y + k, SIDE) * SIDE for k in range(SIDE)]
+    low = [lax.rem(z + k, SIDE) for k in range(SIDE)]
+    offsets = [(a, b, c) for a in range(SIDE) for b in range(SIDE) for c in range(SIDE)][1:]
+    offsets.sort(key=lambda o: -sum(min(k, SIDE - k) for k in o))
 
     barrier = pltpu.get_barrier_semaphore()
     pl.semaphore_signal(barrier, inc=1, device_id=(me, 1 - t), device_id_type=MESH)
@@ -76,9 +84,9 @@
     load_w = [load(w_out.at[w_rows(k), :], wv.at[k], 4 + k) for k in (1, 2, 3)]
     load_in = [load(w_in, wbuf.at[t], 8), load(b_in, bbuf.at[t], 9)]
     load_lat = [load(noise, nz, 10), load(enc_mean, em, 11), load(enc_ls, el, 12)]
-    for c in [load_pls, load_w0[0], load_w0[1], load_b, load_img, load_w[0]]:
+    for c in [load_pls, load_w0[0], load_w0[1], load_w[0], load_w[1], load_w[2], load_b, load_img]:
         c.start()
-    for c in load_in + load_lat + load_w[1:]:
+    for c in load_in + load_lat:
         c.start()
 
     def piece(c):
@@ -118,11 +126,16 @@
             beside(c)
         return a, b
 
+    def part(c, q, lo, n):
+        if q < 5:
+            return gbuf.at[c, q, pl.ds(lo, n), :]
+        return cbuf.at[c, pl.ds((q - 5) * height + lo, n), :]
+
     def exchange(q):
         out = []
         for d in range(6):
             lo, n = G_ROWS[d] if q < 5 else C_ROWS[d]
-            mine = gbuf.at[color, q, pl.ds(lo, n), :] if q < 5 else cbuf.at[color, pl.ds(lo, n), :]
+            mine = part(color, q, lo, n)
             out.append(
                 pltpu.make_async_remote_copy(
                     src_ref=mine, dst_ref=mine, send_sem=g_send.at[q, d], recv_sem=g_recv.at[q, d],
@@ -135,8 +148,7 @@
         out = []
         for d in range(6):
             lo, n = G_ROWS[d] if q < 5 else C_ROWS[d]
-            c = 1 - color
-            ref = gbuf.at[c, q, pl.ds(lo, n), :] if q < 5 else cbuf.at[c, pl.ds(lo, n), :]
+            ref = part(1 - color, q, lo, n)
             out.append(
                 pltpu.make_async_remote_copy(
                     src_ref=ref, dst_ref=ref, send_sem=g_send.at[q, d], recv_sem=g_recv.at[q, d],
@@ -145,7 +157,7 @@
             )
         return out
 
-    all_sends = [exchange(q) for q in range(6)]
+    all_sends = [exchange(q) for q in range(7)]
 
     def send(q):
         for c in all_sends[q]:
@@ -177,27 +189,10 @@
     half_gram(0)
     load_w0[1].wait()
     half_gram(1)
-    for c in load_in:
-        c.wait()
-    pl.semaphore_wait(barrier, 10)
-
-    def pair_copy(ref, k):
-        return pltpu.make_async_remote_copy(
-            src_ref=ref, dst_ref=ref, send_sem=pair_send.at[k], recv_sem=pair_recv.at[k],
-            device_id=(me, 1 - t), device_id_type=MESH,
-        )
-
-    weights, biases = pair_copy(wbuf.at[t], 0), pair_copy(bbuf.at[t], 1)
-    weights.start()
-    biases.start()
-    send(0)
-    load_b.wait()
-    load_img.wait()
     load_w[0].wait()
     def beside_gram(c):
         if c + 1 < chunks:
             scale(1, c + 1)
-        differences(c)
 
     rhs1 = lambda cols: wv[1, :, cols]
 
@@ -208,14 +203,59 @@
         gbuf[color, 1] = g1.astype(BF16)
         gbuf[color, 2] = (0.5 * g2).astype(BF16)
 
+    for c in load_in:
+        c.wait()
+    pl.semaphore_wait(barrier, 10)
+
+    def pair_copy(ref, k):
+        return pltpu.make_async_remote_copy(
+            src_ref=ref, dst_ref=ref, send_sem=pair_send.at[k], recv_sem=pair_recv.at[k],
+            device_id=(me, 1 - t), device_id_type=MESH,
+        )
+
+    weights, biases = pair_copy(wbuf.at[t], 0), pair_copy(bbuf.at[t], 1)
+    weights.start()
+    biases.start()
+    for other in line["y"]:
+        pl.semaphore_signal(plane_sem, inc=1, device_id=(other, t), device_id_type=MESH)
+    send(0)
     send(1)
     send(2)
+    load_w[1].wait()
+    load_w[2].wait()
+    load_b.wait()
+    load_img.wait()
+    rhs2, rhs3 = (lambda cols: wv[2, :, cols]), (lambda cols: wv[3, :, cols])
+
+    @block
+    def _():
+        g3, g4 = two_grams((ws, 0, rhs2), (ws, 1, rhs3), differences)
+        gbuf[color, 3] = g3.astype(BF16)
+        gbuf[color, 4] = g4.astype(BF16)
+
+    send(3)
+    send(4)
+    pl.semaphore_wait(plane_sem, 3)
+    for other in line["z"]:
+        pl.semaphore_signal(cube_sem, inc=1, device_id=(other, t), device_id_type=MESH)
     for c in load_lat:
         c.wait()
-    rhs_d = lambda cols: dv[:, cols]
-
-    @block
-    def _():
+
+    def cross(k, beside):
+        @block
+        def _():
+            aside = beside()
+            parts = [None, None]
+            for c in range(chunks):
+                cols = piece(c)
+                parts[c % 2] = plus(parts[c % 2], nt(wv[k, :, cols], dv[:, cols]))
+                aside(c)
+            both = parts[0] + parts[1]
+            cbuf[color, k * 256 : (k + 1) * 256, :] = both[:, 0:128] + both[:, 128:256]
+
+        send(5 + k)
+
+    def latents():
         mean_t = em[...].T
         ls_t = el[...].T
         exp_t = jnp.exp(ls_t)
@@ -223,7 +263,7 @@
         first_row = lax.broadcasted_iota(jnp.int32, (128, 1024), 0) == 0
         lat[128:256, :] = jnp.where(first_row, 1.0, 0.0).astype(BF16)
 
-        def beside_cross(c):
+        def aside(c):
             if c < 8:
                 n_t = nz[pl.ds(c, 128, stride=8), :].T
                 l_t = mean_t + exp_t * n_t
@@ -231,35 +271,25 @@
                 squares = jnp.sum(n_t * n_t - l_t * l_t, axis=0, keepdims=True)
                 pp[c : c + 1, :] = 0.5 * squares + ls_sum
 
-        c1, c2 = two_grams((wv, 0, rhs_d), (wv, 1, rhs_d), beside_cross)
-        cbuf[color, 0:256, :] = c1[:, 0:128] + c1[:, 128:256]
-        cbuf[color, 256:512, :] = c2[:, 0:128] + c2[:, 128:256]
-
-    send(5)
+        return aside
+
+    def projections():
+        row0 = lax.broadcasted_iota(jnp.int32, (128, 128), 0) == 0
+
+        def aside(c):
+            if c < 8:
+                k, lo = c // 4, (c % 4) * 128
+                rows = slice(c * 128, (c + 1) * 128)
+                wat[rows, 0:128] = wbuf[k, :, lo : lo + 128].astype(F32).T.astype(BF16)
+                bias = jnp.where(row0, bbuf[k, :, lo : lo + 128].astype(F32), 0.0)
+                wat[rows, 128:256] = bias.T.astype(BF16)
+
+        return aside
+
+    cross(0, latents)
     pair_copy(wbuf.at[1 - t], 0).wait_recv()
     pair_copy(bbuf.at[1 - t], 1).wait_recv()
-    load_w[1].wait()
-    load_w[2].wait()
-    row0 = lax.broadcasted_iota(jnp.int32, (128, 128), 0) == 0
-
-    def beside_last(c):
-        if c < 8:
-            k, lo = c // 4, (c % 4) * 128
-            rows = slice(c * 128, (c + 1) * 128)
-            wat[rows, 0:128] = wbuf[k, :, lo : lo + 128].astype(F32).T.astype(BF16)
-            bias = jnp.where(row0, bbuf[k, :, lo : lo + 128].astype(F32), 0.0)
-            wat[rows, 128:256] = bias.T.astype(BF16)
-
-    rhs2, rhs3 = (lambda cols: wv[2, :, cols]), (lambda cols: wv[3, :, cols])
-
-    @block
-    def _():
-        g3, g4 = two_grams((ws, 0, rhs2), (ws, 1, rhs3), beside_last)
-        gbuf[color, 3] = g3.astype(BF16)
-        gbuf[color, 4] = g4.astype(BF16)
-
-    send(3)
-    send(4)
+    cross(1, projections)
     @block
     def _():
         for k in range(4):
@@ -305,7 +335,7 @@
     block(functools.partial(apply, color, 0))
     image_part = -0.5 * jnp.sum(acc_sq[...].T, axis=0, keepdims=True)
     lsend[8:16, :] = jnp.broadcast_to(image_part - total_ls - pixels * HALF_LOG_TAU, (8, 128))
-    for q in (0, 1, 2, 5, 3, 4):
+    for q in range(7):
         for c in arrivals(q):
             c.wait_recv()
     block(functools.partial(apply, 1 - color, 1))
@@ -315,45 +345,45 @@
         device_id=(me, 1 - t), device_id_type=MESH,
     )
     share.start()
+    pl.semaphore_wait(cube_sem, 3)
     share.wait_recv()
     loglik = lsend[...] + lrecv[...]
     image_term = loglik[8:9, :]
     logw = loglik[0:8, :] + pp[...]
     peak = jnp.max(logw, axis=0, keepdims=True)
     sums = jnp.sum(jnp.exp(logw - peak), axis=0, keepdims=True)
-    rounds = []
-    for r, axis in enumerate(("z", "y", "x")):
-        sbuf[r, 0:1, :] = peak
-        sbuf[r, 1:2, :] = sums
-        copies = [
-            pltpu.make_async_remote_copy(
-                src_ref=sbuf.at[r], dst_ref=rbuf.at[r, k], send_sem=x_send.at[r, k],
-                recv_sem=x_recv.at[r, k], device_id=(line[axis][k], t), device_id_type=MESH,
-            )
-            for k in range(3)
-        ]
-        for c in copies:
-            c.start()
-        for c in copies:
-            c.wait_recv()
-        rounds += copies
-        top = peak
-        for k in range(3):
-            top = jnp.maximum(top, rbuf[r, k, 0:1, :])
-        sums = sums * jnp.exp(peak - top)
-        for k in range(3):
-            sums += rbuf[r, k, 1:2, :] * jnp.exp(rbuf[r, k, 0:1, :] - top)
-        peak = top
+    sbuf[0:1, :] = peak
+    sbuf[1:2, :] = sums
+    for k, (a, b, c) in enumerate(offsets):
+        pltpu.make_async_remote_copy(
+            src_ref=sbuf, dst_ref=rbuf.at[me], send_sem=x_send, recv_sem=x_recv,
+            device_id=(far[a] + mid[b] + low[c], t), device_id_type=MESH,
+        ).start()
+    rbuf[me] = sbuf[...]
+    others = rbuf.at[pl.ds(0, len(offsets))]
+    pltpu.make_async_copy(others, others, x_recv).wait()
+    top = peak
+    for k in range(len(offsets) + 1):
+        top = jnp.maximum(top, rbuf[k, 0:1, :])
+    sums = jnp.zeros_like(peak)
+    for k in range(len(offsets) + 1):
+        sums += rbuf[k, 1:2, :] * jnp.exp(rbuf[k, 0:1, :] - top)
     log_sum = jnp.log(sums)
     log_all = math.log(all_samples)
-    bound_ref[...] = (image_term + peak + log_sum - log_all) / all_pixels
-    lw_ref[...] = logw - peak - log_sum + log_all
-
-    for c in rounds + [share, weights, biases]:
+    out_ref[0:8, :] = logw - top - log_sum + log_all
+    out_ref[8:16, :] = jnp.broadcast_to((image_term + top + log_sum - log_all) / all_pixels, (8, 128))
+
+    pltpu.make_async_copy(others, others, x_send).wait()
+    for c in [share, weights, biases]:
         c.wait_send()
-    for q in range(6):
+    for q in range(7):
         for c in all_sends[q]:
             c.wait_send()
+
+
+def finish(out_ref, bound_ref, lw_ref):
+    bound_ref[...] = out_ref[8:9, :]
+    lw_ref[...] = out_ref[0:8, :]
 
 
 def on_device(images, enc_mean, enc_logscale, noise, w_in, b_in, w_out, b_out, pixel_logscale):
@@ -363,14 +393,11 @@
     noise = noise.reshape(image_count * sample_count, latent_dims)
     half = w_in.shape[1]
     V = pltpu.VMEM
-    bound, lw = pl.pallas_call(
+    outputs = pl.pallas_call(
         kernel,
-        out_shape=(
-            jax.ShapeDtypeStruct((1, image_count), F32),
-            jax.ShapeDtypeStruct((sample_count, image_count), F32),
-        ),
+        out_shape=FINAL((16, image_count), F32),
         in_specs=[pl.BlockSpec(memory_space=pl.ANY)] * 9,
-        out_specs=[pl.BlockSpec(memory_space=pltpu.VMEM)] * 2,
+        out_specs=pl.BlockSpec(memory_space=pltpu.VMEM),
         scratch_shapes=[
             V((4, height, pixels), BF16), V((2, height, pixels), BF16), V((image_count, pixels), BF16),
             V((2 * image_count, pixels), BF16), V((1, pixels), F32), V((1, pixels), F32),
@@ -380,15 +407,25 @@
             V((2, 5, height, height), BF16), V((2, 2 * height, image_count), F32),
             V((height, height), F32), V((1, pixels), F32), V((image_count, 128), F32), V((sample_count, image_count), F32),
             V((16, image_count), F32), V((16, image_count), F32),
-            V((3, 8, image_count), F32), V((3, 3, 8, image_count), F32),
-            pltpu.SemaphoreType.DMA((13,)), pltpu.SemaphoreType.DMA((6, 6)), pltpu.SemaphoreType.DMA((6, 6)),
+            V((2, image_count), F32), V((64, 2, image_count), F32),
+            pltpu.SemaphoreType.DMA((13,)), pltpu.SemaphoreType.DMA((7, 6)), pltpu.SemaphoreType.DMA((7, 6)),
             pltpu.SemaphoreType.DMA((3,)), pltpu.SemaphoreType.DMA((3,)),
-            pltpu.SemaphoreType.DMA((3, 3)), pltpu.SemaphoreType.DMA((3, 3)),
+            pltpu.SemaphoreType.DMA, pltpu.SemaphoreType.DMA,
+            pltpu.SemaphoreType.REGULAR, pltpu.SemaphoreType.REGULAR,
         ],
         compiler_params=pltpu.CompilerParams(
             collective_id=0, has_side_effects=True, vmem_limit_bytes=60 * 1024 * 1024
         ),
     )(images, enc_mean, enc_logscale, noise, w_in, b_in, w_out, b_out, pixel_logscale)
+    bound, lw = pl.pallas_call(
+        finish,
+        out_shape=(
+            jax.ShapeDtypeStruct((1, image_count), F32),
+            jax.ShapeDtypeStruct((sample_count, image_count), F32),
+        ),
+        in_specs=[pl.BlockSpec(memory_space=pltpu.VMEM)],
+        out_specs=[pl.BlockSpec(memory_space=pltpu.VMEM)] * 2,
+    )(pltpu.with_memory_space_constraint(outputs, pltpu.VMEM))
     return bound.reshape(image_count), lw.T
 
 

time: 34.5 us -> 28.9 us (0.84)
  the two profiles are of different devices: /device:TPU:0 before, /device:TPU:1 now
where the time goes in v3:
time: 28.9 us; the launch traced here: 28.8 us
  Pallas kernels  28.2 us (98%)
  between operations  0.64 us (2%)
    pallas_call x1, Pallas kernels, on_device(): pl.pallas_call(kernel, out_shape=FINAL((16, image_count), F32), in_specs=...  27.6 us
    pallas_call x1, Pallas kernels, on_device(): pl.pallas_call(finish, out_shape=(jax.ShapeDtypeStruct((1, image_count),...  0.6 us

profile of v3, /device:TPU:1, one launch (start us, length us, event | category | flops | bytes accessed | tf_op | source)
XLA Modules:
  0.0 28.8 jit_solution(8320851658914397552)
XLA Ops:
  0.6 27.6 %shard_map.104.out_ref = f32[16,128]{1,0:T(8,128)S(1)} custom-call(bf16[128,6144]{1,0:T(8,128)(2,1)} %images.1, f32[128,128]{1,0:T(8,128)} %enc_mean.1, f32[128,128]{1,0:T(8,128)} %enc_ls.1, f32[1024,128]{1,0:T(8,128)} %bitcast.3, bf16[128,512]{1,0:T(8,128)(2,1)} %w_in.1, bf16[1,512]{1,0:T(2,128)(2,1)} %b_in.1, bf16[1024,6144]{1,0:T(8,128)(2,1)} %w_out.1, ...), custom_call_target="tpu_custom_call" | custom-call | tf_op jit(solution)/shard_map/pallas_call | solution.py:396
  28.2 0.6 %shard_map.105 = (f32[1,128]{1,0:T(1,128)}, f32[8,128]{1,0:T(8,128)}) custom-call(f32[16,128]{1,0:T(8,128)S(1)} %shard_map.104.out_ref), custom_call_target="tpu_custom_call" | custom-call | tf_op jit(solution)/shard_map/pallas_call | solution.py:420

commit v4 on v3

--- a/solution.py
+++ b/solution.py
@@ -13,8 +13,6 @@
 F32 = jnp.float32
 BF16 = jnp.bfloat16
 NT = (((1,), (1,)), ((), ()))
-G_ROWS = ((0, 48), (48, 48), (96, 48), (144, 48), (192, 32), (224, 32))
-C_ROWS = ((0, 48), (48, 48), (96, 40), (136, 40), (176, 40), (216, 40))
 SIDE = 4
 FINAL = pltpu.VMEM
 
@@ -22,7 +20,7 @@
 def kernel(
     images, enc_mean, enc_ls, noise, w_in, b_in, w_out, b_out, pls,
     out_ref,
-    wv, ws, img, dv, bv, pv, nz, em, el, wbuf, bbuf, wat, lat, hid, gbuf, cbuf,
+    wv, ws, img, dv, bv, pv, nz, em, el, wbuf, bbuf, wat, lat, hid, gbuf, cbuf, lbuf,
     g_half, s2v, acc_sq, pp, lsend, lrecv, sbuf, rbuf,
     in_sem, g_send, g_recv, pair_send, pair_recv, x_send, x_recv,
     plane_sem, cube_sem,
@@ -30,7 +28,7 @@
     me = lax.axis_index("samp")
     t = lax.axis_index("tp")
     x, y, z = me // (SIDE * SIDE), (me // SIDE) % SIDE, me % SIDE
-    color = (x + y + z) % 2
+    color = (x + 2 * y + z) % SIDE
     pixels = img.shape[1]
     all_pixels = 2 * pixels
     all_samples = 8 * SIDE * SIDE * SIDE
@@ -60,10 +58,7 @@
         for other in line[axis]:
             pl.semaphore_signal(barrier, inc=1, device_id=(other, t), device_id_type=MESH)
 
-    def slabs(p):
-        return 2 * p, 2 * p + 1, 2 - p, 3 - 3 * p
-
-    own = slabs(color)
+    own = [lax.rem(color + k, SIDE) for k in range(SIDE)]
     height = wv.shape[1]
     step = 512
     chunks = pixels // step
@@ -84,9 +79,7 @@
     load_w = [load(w_out.at[w_rows(k), :], wv.at[k], 4 + k) for k in (1, 2, 3)]
     load_in = [load(w_in, wbuf.at[t], 8), load(b_in, bbuf.at[t], 9)]
     load_lat = [load(noise, nz, 10), load(enc_mean, em, 11), load(enc_ls, el, 12)]
-    for c in [load_pls, load_w0[0], load_w0[1], load_w[0], load_w[1], load_w[2], load_b, load_img]:
-        c.start()
-    for c in load_in + load_lat:
+    for c in [load_pls] + load_w0 + load_in + [load_b, load_img] + load_lat + load_w:
         c.start()
 
     def piece(c):
@@ -117,51 +110,28 @@
     def plus(total, more):
         return more if total is None else total + more
 
-    def two_grams(first, second, beside):
-        a = b = None
-        for c in range(chunks):
-            cols = piece(c)
-            a = plus(a, nt(first[0][first[1], :, cols], first[2](cols)))
-            b = plus(b, nt(second[0][second[1], :, cols], second[2](cols)))
-            beside(c)
-        return a, b
-
-    def part(c, q, lo, n):
-        if q < 5:
-            return gbuf.at[c, q, pl.ds(lo, n), :]
-        return cbuf.at[c, pl.ds((q - 5) * height + lo, n), :]
-
-    def exchange(q):
-        out = []
-        for d in range(6):
-            lo, n = G_ROWS[d] if q < 5 else C_ROWS[d]
-            mine = part(color, q, lo, n)
-            out.append(
-                pltpu.make_async_remote_copy(
-                    src_ref=mine, dst_ref=mine, send_sem=g_send.at[q, d], recv_sem=g_recv.at[q, d],
-                    device_id=(near[d], t), device_id_type=MESH,
-                )
-            )
-        return out
-
-    def arrivals(q):
-        out = []
-        for d in range(6):
-            lo, n = G_ROWS[d] if q < 5 else C_ROWS[d]
-            ref = part(1 - color, q, lo, n)
-            out.append(
-                pltpu.make_async_remote_copy(
-                    src_ref=ref, dst_ref=ref, send_sem=g_send.at[q, d], recv_sem=g_recv.at[q, d],
-                    device_id=(near[d], t), device_id_type=MESH,
-                )
-            )
-        return out
-
-    all_sends = [exchange(q) for q in range(7)]
+    halves = (0, 0, 0, 1, 1, 1)
+    senders = [own[k] for k in (3, 1, 2, 2, 3, 1)]
+
+    def part(c, q, d):
+        rows = pl.ds(halves[d] * (height // 2), height // 2)
+        return gbuf.at[c, q, rows, :] if q < 2 else cbuf.at[c, rows, :]
+
+    def to_near(ref, q, d):
+        return pltpu.make_async_remote_copy(
+            src_ref=ref, dst_ref=ref, send_sem=g_send.at[q, d], recv_sem=g_recv.at[q, d],
+            device_id=(near[d], t), device_id_type=MESH,
+        )
+
+    all_sends = [[to_near(part(color, q, d), q, d) for d in range(6)] for q in range(3)]
 
     def send(q):
         for c in all_sends[q]:
             c.start()
+
+    def receive(q):
+        for d in range(6):
+            to_near(part(senders[d], q, d), q, d).wait_recv()
 
     load_pls.wait()
     s2v[...] = jnp.exp(-2.0 * pv[...])
@@ -189,20 +159,6 @@
     half_gram(0)
     load_w0[1].wait()
     half_gram(1)
-    load_w[0].wait()
-    def beside_gram(c):
-        if c + 1 < chunks:
-            scale(1, c + 1)
-
-    rhs1 = lambda cols: wv[1, :, cols]
-
-    @block
-    def _():
-        scale(1, 0)
-        g1, g2 = two_grams((ws, 0, rhs1), (ws, 1, rhs1), beside_gram)
-        gbuf[color, 1] = g1.astype(BF16)
-        gbuf[color, 2] = (0.5 * g2).astype(BF16)
-
     for c in load_in:
         c.wait()
     pl.semaphore_wait(barrier, 10)
@@ -216,80 +172,79 @@
     weights, biases = pair_copy(wbuf.at[t], 0), pair_copy(bbuf.at[t], 1)
     weights.start()
     biases.start()
+    send(0)
     for other in line["y"]:
         pl.semaphore_signal(plane_sem, inc=1, device_id=(other, t), device_id_type=MESH)
-    send(0)
-    send(1)
-    send(2)
-    load_w[1].wait()
-    load_w[2].wait()
     load_b.wait()
     load_img.wait()
-    rhs2, rhs3 = (lambda cols: wv[2, :, cols]), (lambda cols: wv[3, :, cols])
-
-    @block
-    def _():
-        g3, g4 = two_grams((ws, 0, rhs2), (ws, 1, rhs3), differences)
-        gbuf[color, 3] = g3.astype(BF16)
-        gbuf[color, 4] = g4.astype(BF16)
-
-    send(3)
-    send(4)
-    pl.semaphore_wait(plane_sem, 3)
-    for other in line["z"]:
-        pl.semaphore_signal(cube_sem, inc=1, device_id=(other, t), device_id_type=MESH)
+
+    @block
+    def _():
+        parts = [None, None]
+        differences(0)
+        differences(1)
+        for c in range(chunks):
+            cols = piece(c)
+            parts[c % 2] = plus(parts[c % 2], nt(wv[0, :, cols], dv[:, cols]))
+            if c + 2 < chunks:
+                differences(c + 2)
+        both = parts[0] + parts[1]
+        cbuf[color] = both[:, 0:128] + both[:, 128:256]
+
+    send(2)
     for c in load_lat:
         c.wait()
-
-    def cross(k, beside):
-        @block
-        def _():
-            aside = beside()
-            parts = [None, None]
-            for c in range(chunks):
-                cols = piece(c)
-                parts[c % 2] = plus(parts[c % 2], nt(wv[k, :, cols], dv[:, cols]))
-                aside(c)
-            both = parts[0] + parts[1]
-            cbuf[color, k * 256 : (k + 1) * 256, :] = both[:, 0:128] + both[:, 128:256]
-
-        send(5 + k)
-
-    def latents():
+    load_w[0].wait()
+
+    @block
+    def _():
         mean_t = em[...].T
         ls_t = el[...].T
         exp_t = jnp.exp(ls_t)
         ls_sum = jnp.sum(ls_t, axis=0, keepdims=True)
         first_row = lax.broadcasted_iota(jnp.int32, (128, 1024), 0) == 0
         lat[128:256, :] = jnp.where(first_row, 1.0, 0.0).astype(BF16)
-
-        def aside(c):
+        parts = [None, None]
+        for c in range(chunks):
+            cols = piece(c)
+            parts[c % 2] = plus(parts[c % 2], nt(ws[0, :, cols], wv[1, :, cols]))
             if c < 8:
                 n_t = nz[pl.ds(c, 128, stride=8), :].T
                 l_t = mean_t + exp_t * n_t
                 lat[0:128, c * 128 : (c + 1) * 128] = l_t.astype(BF16)
                 squares = jnp.sum(n_t * n_t - l_t * l_t, axis=0, keepdims=True)
                 pp[c : c + 1, :] = 0.5 * squares + ls_sum
-
-        return aside
-
-    def projections():
+        gbuf[color, 1] = (parts[0] + parts[1]).astype(BF16)
+
+    send(1)
+    pl.semaphore_wait(plane_sem, 3)
+    for other in line["z"]:
+        pl.semaphore_signal(cube_sem, inc=1, device_id=(other, t), device_id_type=MESH)
+    pair_copy(wbuf.at[1 - t], 0).wait_recv()
+    pair_copy(bbuf.at[1 - t], 1).wait_recv()
+    load_w[1].wait()
+    load_w[2].wait()
+
+    @block
+    def _():
         row0 = lax.broadcasted_iota(jnp.int32, (128, 128), 0) == 0
-
-        def aside(c):
+        l0 = l1 = None
+        scale(1, 0)
+        for c in range(chunks):
+            cols = piece(c)
+            l0 = plus(l0, nt(ws[0, :, cols], wv[2, :, cols]))
+            l1 = plus(l1, nt(ws[1, :, cols], wv[3, :, cols]))
+            if c + 1 < chunks:
+                scale(1, c + 1)
             if c < 8:
                 k, lo = c // 4, (c % 4) * 128
                 rows = slice(c * 128, (c + 1) * 128)
                 wat[rows, 0:128] = wbuf[k, :, lo : lo + 128].astype(F32).T.astype(BF16)
                 bias = jnp.where(row0, bbuf[k, :, lo : lo + 128].astype(F32), 0.0)
                 wat[rows, 128:256] = bias.T.astype(BF16)
-
-        return aside
-
-    cross(0, latents)
-    pair_copy(wbuf.at[1 - t], 0).wait_recv()
-    pair_copy(bbuf.at[1 - t], 1).wait_recv()
-    cross(1, projections)
+        lbuf[0] = l0.astype(BF16)
+        lbuf[1] = l1.astype(BF16)
+
     @block
     def _():
         for k in range(4):
@@ -298,47 +253,52 @@
             hid[k] = jnp.maximum(pre, 0.0).astype(BF16)
 
 
-    def apply(p, which):
-        o1, o2, x1, x2 = slabs(p)
+    def against(ref, k, cols):
+        return jnp.dot(ref, hid[own[k], :, cols], preferred_element_type=F32)
+
+    def weigh(y, k, cols):
+        h = hid[own[k], :, cols].astype(F32)
+        c = cbuf[own[k]]
+        return jnp.sum((jnp.concatenate([c, c], axis=1) - y) * h, axis=0, keepdims=True)
+
+    def rows_of(total, n, first):
+        for h in range(2):
+            s = 2 * n + h
+            lanes = total[:, h * 128 : (h + 1) * 128]
+            if first:
+                lsend[s : s + 1, :] = lanes
+            else:
+                lsend[s : s + 1, :] += lanes
+
+    @block
+    def _():
         for n in range(4):
             cols = slice(n * 256, (n + 1) * 256)
 
-            def long():
-                y = jnp.dot(gbuf[p, 0], hid[o1, :, cols], preferred_element_type=F32)
-                y += jnp.dot(gbuf[p, 1], hid[o2, :, cols], preferred_element_type=F32)
-                return y + jnp.dot(gbuf[p, 3], hid[x1, :, cols], preferred_element_type=F32)
-
-            def short():
-                y = jnp.dot(gbuf[p, 2], hid[o2, :, cols], preferred_element_type=F32)
-                return y + jnp.dot(gbuf[p, 4], hid[x2, :, cols], preferred_element_type=F32)
-
-            if n % 2 == 0:
-                y1 = long()
-                y2 = short()
-            else:
-                y2 = short()
-                y1 = long()
-            for h in range(2):
-                s = 2 * n + h
-                part = slice(h * 128, (h + 1) * 128)
-                lanes = slice(s * 128, (s + 1) * 128)
-                total = jnp.sum(
-                    (cbuf[p, 0:256, :] - y1[:, part]) * hid[o1, :, lanes].astype(F32)
-                    + (cbuf[p, 256:512, :] - y2[:, part]) * hid[o2, :, lanes].astype(F32),
-                    axis=0, keepdims=True,
-                )
-                if which == 0:
-                    lsend[s : s + 1, :] = total
-                else:
-                    lsend[s : s + 1, :] += total
-
-    block(functools.partial(apply, color, 0))
+            def two(first, k, second, j):
+                return against(first, k, cols) + against(second, j, cols)
+
+            y = two(gbuf[color, 0], 0, gbuf[color, 1], 1)
+            w = against(lbuf[0], 2, cols)
+            v = against(lbuf[1], 3, cols)
+            far_part = jnp.sum(v * hid[own[1], :, cols].astype(F32), axis=0, keepdims=True)
+            rows_of(weigh(y + w, 0, cols) - far_part, n, True)
+
     image_part = -0.5 * jnp.sum(acc_sq[...].T, axis=0, keepdims=True)
     lsend[8:16, :] = jnp.broadcast_to(image_part - total_ls - pixels * HALF_LOG_TAU, (8, 128))
-    for q in range(7):
-        for c in arrivals(q):
-            c.wait_recv()
-    block(functools.partial(apply, 1 - color, 1))
+    for q in (0, 2, 1):
+        receive(q)
+
+    @block
+    def _():
+        for n in range(4):
+            cols = slice(n * 256, (n + 1) * 256)
+            total = None
+            for k in (1, 2, 3):
+                c = own[k]
+                y = against(gbuf[c, 0], k, cols) + against(gbuf[c, 1], (k + 1) % 4, cols)
+                total = plus(total, weigh(y, k, cols))
+            rows_of(total, n, False)
 
     share = pltpu.make_async_remote_copy(
         src_ref=lsend, dst_ref=lrecv, send_sem=pair_send.at[2], recv_sem=pair_recv.at[2],
@@ -376,7 +336,7 @@
     pltpu.make_async_copy(others, others, x_send).wait()
     for c in [share, weights, biases]:
         c.wait_send()
-    for q in range(7):
+    for q in range(3):
         for c in all_sends[q]:
             c.wait_send()
 
@@ -404,11 +364,11 @@
             V(noise.shape, F32), V((image_count, latent_dims), F32), V((image_count, latent_dims), F32),
             V((2, latent_dims, half), BF16), V((2, 1, half), BF16), V((hidden, 256), BF16),
             V((256, image_count * sample_count), BF16), V((4, height, image_count * sample_count), BF16),
-            V((2, 5, height, height), BF16), V((2, 2 * height, image_count), F32),
+            V((4, 2, height, height), BF16), V((4, height, image_count), F32), V((2, height, height), BF16),
             V((height, height), F32), V((1, pixels), F32), V((image_count, 128), F32), V((sample_count, image_count), F32),
             V((16, image_count), F32), V((16, image_count), F32),
             V((2, image_count), F32), V((64, 2, image_count), F32),
-            pltpu.SemaphoreType.DMA((13,)), pltpu.SemaphoreType.DMA((7, 6)), pltpu.SemaphoreType.DMA((7, 6)),
+            pltpu.SemaphoreType.DMA((13,)), pltpu.SemaphoreType.DMA((3, 6)), pltpu.SemaphoreType.DMA((3, 6)),
             pltpu.SemaphoreType.DMA((3,)), pltpu.SemaphoreType.DMA((3,)),
             pltpu.SemaphoreType.DMA, pltpu.SemaphoreType.DMA,
             pltpu.SemaphoreType.REGULAR, pltpu.SemaphoreType.REGULAR,

time: 28.9 us -> 24.8 us (0.86)
  Pallas kernels: 28.2 us -> 24 us
    pallas_call x1, Pallas kernels: 27.6 us -> 23.4 us  [on_device(): pl.pallas_call(kernel, out_shape=FINAL((16, image_count), F32), in_specs=...]
where the time goes in v4:
time: 24.8 us; the launch traced here: 24.7 us
  Pallas kernels  24 us (97%)
  between operations  0.64 us (3%)
    pallas_call x1, Pallas kernels, on_device(): pl.pallas_call(kernel, out_shape=FINAL((16, image_count), F32), in_specs=...  23.4 us
    pallas_call x1, Pallas kernels, on_device(): pl.pallas_call(finish, out_shape=(jax.ShapeDtypeStruct((1, image_count),...  0.6 us

profile of v4, /device:TPU:1, one launch (start us, length us, event | category | flops | bytes accessed | tf_op | source)
XLA Modules:
  0.0 24.7 jit_solution(7530300166891760942)
XLA Ops:
  0.6 23.4 %shard_map.104.out_ref = f32[16,128]{1,0:T(8,128)S(1)} custom-call(bf16[128,6144]{1,0:T(8,128)(2,1)} %images.1, f32[128,128]{1,0:T(8,128)} %enc_mean.1, f32[128,128]{1,0:T(8,128)} %enc_ls.1, f32[1024,128]{1,0:T(8,128)} %bitcast.3, bf16[128,512]{1,0:T(8,128)(2,1)} %w_in.1, bf16[1,512]{1,0:T(2,128)(2,1)} %b_in.1, bf16[1024,6144]{1,0:T(8,128)(2,1)} %w_out.1, ...), custom_call_target="tpu_custom_call" | custom-call | tf_op jit(solution)/shard_map/pallas_call | solution.py:356
  24.1 0.6 %shard_map.105 = (f32[1,128]{1,0:T(1,128)}, f32[8,128]{1,0:T(8,128)}) custom-call(f32[16,128]{1,0:T(8,128)S(1)} %shard_map.104.out_ref), custom_call_target="tpu_custom_call" | custom-call | tf_op jit(solution)/shard_map/pallas_call | solution.py:380

commit v5 on v4

--- a/solution.py
+++ b/solution.py
@@ -20,8 +20,8 @@
 def kernel(
     images, enc_mean, enc_ls, noise, w_in, b_in, w_out, b_out, pls,
     out_ref,
-    wv, ws, img, dv, bv, pv, nz, em, el, wbuf, bbuf, wat, lat, hid, gbuf, cbuf, lbuf,
-    g_half, s2v, acc_sq, pp, lsend, lrecv, sbuf, rbuf,
+    wv, ws, img, dv, row, nz, wbuf, bbuf, wat, lat, hid, gbuf, cbuf, lbuf,
+    g_part, s2v, acc_sq, pp, lsend, lrecv, sbuf, rbuf,
     in_sem, g_send, g_recv, pair_send, pair_recv, x_send, x_recv,
     plane_sem, cube_sem,
 ):
@@ -50,7 +50,40 @@
     mid = [lax.rem(y + k, SIDE) * SIDE for k in range(SIDE)]
     low = [lax.rem(z + k, SIDE) for k in range(SIDE)]
     offsets = [(a, b, c) for a in range(SIDE) for b in range(SIDE) for c in range(SIDE)][1:]
-    offsets.sort(key=lambda o: -sum(min(k, SIDE - k) for k in o))
+    offsets.sort(key=lambda o: sum((k + 3) % SIDE for k in o))
+
+    own = [lax.rem(color + k, SIDE) for k in range(SIDE)]
+    height = wv.shape[1]
+    step = 512
+    chunks = pixels // step
+
+    def load(src, dst, k):
+        return pltpu.make_async_copy(src, dst, in_sem.at[k])
+
+    def w_rows(k):
+        return pl.ds(pl.multiple_of(own[k] * height, height), height)
+
+    cuts = (0, 2, 6, chunks)
+    load_row = [load(pls, row.at[0], 0), load(b_out, row.at[1], 0)]
+    load_first = [
+        load(
+            w_out.at[w_rows(0), pl.ds(cuts[k] * step, (cuts[k + 1] - cuts[k]) * step)],
+            wv.at[0, :, pl.ds(cuts[k] * step, (cuts[k + 1] - cuts[k]) * step)],
+            1 + k,
+        )
+        for k in range(3)
+    ]
+    load_in = [load(w_in, wbuf.at[t], 4), load(b_in, bbuf.at[t], 5)]
+    load_img = load(images, img, 6)
+    images_n, samples_n = enc_mean.shape[0], noise.shape[0]
+    load_lat = [
+        load(noise, nz.at[pl.ds(0, samples_n), :], 7),
+        load(enc_mean, nz.at[pl.ds(samples_n, images_n), :], 7),
+        load(enc_ls, nz.at[pl.ds(samples_n + images_n, images_n), :], 7),
+    ]
+    load_w = [load(w_out.at[w_rows(k), :], wv.at[k], (8, 9, 9)[k - 1]) for k in (1, 2, 3)]
+    for c in load_row + load_first + load_in + [load_img] + load_lat + load_w:
+        c.start()
 
     barrier = pltpu.get_barrier_semaphore()
     pl.semaphore_signal(barrier, inc=1, device_id=(me, 1 - t), device_id_type=MESH)
@@ -58,30 +91,6 @@
         for other in line[axis]:
             pl.semaphore_signal(barrier, inc=1, device_id=(other, t), device_id_type=MESH)
 
-    own = [lax.rem(color + k, SIDE) for k in range(SIDE)]
-    height = wv.shape[1]
-    step = 512
-    chunks = pixels // step
-
-    def load(src, dst, k):
-        return pltpu.make_async_copy(src, dst, in_sem.at[k])
-
-    def w_rows(k):
-        return pl.ds(pl.multiple_of(own[k] * height, height), height)
-
-    load_pls, load_b = load(pls, pv, 0), load(b_out, bv, 1)
-    half = pixels // 2
-    load_w0 = [
-        load(w_out.at[w_rows(0), pl.ds(k * half, half)], wv.at[0, :, pl.ds(k * half, half)], 2 + k)
-        for k in range(2)
-    ]
-    load_img = load(images, img, 4)
-    load_w = [load(w_out.at[w_rows(k), :], wv.at[k], 4 + k) for k in (1, 2, 3)]
-    load_in = [load(w_in, wbuf.at[t], 8), load(b_in, bbuf.at[t], 9)]
-    load_lat = [load(noise, nz, 10), load(enc_mean, em, 11), load(enc_ls, el, 12)]
-    for c in [load_pls] + load_w0 + load_in + [load_b, load_img] + load_lat + load_w:
-        c.start()
-
     def piece(c):
         return slice(c * step, (c + 1) * step)
 
@@ -90,16 +99,25 @@
             cols = slice(c * step + q * 256, c * step + (q + 1) * 256)
             ws[k, :, cols] = wv[k, :, cols] * s2v[:, cols].astype(BF16)
 
-    def differences(c):
+    def differences(q):
+        cols = slice(q * 256, (q + 1) * 256)
+        e = (img[:, cols].astype(F32) - row[1, :, cols]) * s2v[:, cols]
+        hi = e.astype(BF16)
+        dv[0:128, cols] = hi
+        dv[128:256, cols] = (e - hi.astype(F32)).astype(BF16)
+
+    def squares(c):
         for q in range(2):
             cols = slice(c * step + q * 256, c * step + (q + 1) * 256)
-            d = img[:, cols].astype(F32) - bv[:, cols]
-            e = d * s2v[:, cols]
-            hi = e.astype(BF16)
-            dv[0:128, cols] = hi
-            dv[128:256, cols] = (e - hi.astype(F32)).astype(BF16)
-            sq = d * e
+            d = img[:, cols].astype(F32) - row[1, :, cols]
+            sq = d * d * s2v[:, cols]
             acc_sq[...] += sq[:, 0:128] + sq[:, 128:256]
+
+    def project(k, lo):
+        rows = slice(lo, lo + 128)
+        row0 = lax.broadcasted_iota(jnp.int32, (128, 128), 0) == 0
+        wat[k, rows, 0:128] = wbuf[k, :, rows].astype(F32).T.astype(BF16)
+        wat[k, rows, 128:256] = jnp.where(row0, bbuf[k, :, rows].astype(F32), 0.0).T.astype(BF16)
 
     def nt(a, b):
         return lax.dot_general(a, b, NT, preferred_element_type=F32)
@@ -119,7 +137,7 @@
 
     def to_near(ref, q, d):
         return pltpu.make_async_remote_copy(
-            src_ref=ref, dst_ref=ref, send_sem=g_send.at[q, d], recv_sem=g_recv.at[q, d],
+            src_ref=ref, dst_ref=ref, send_sem=g_send, recv_sem=g_recv.at[q],
             device_id=(near[d], t), device_id_type=MESH,
         )
 
@@ -129,19 +147,21 @@
         for c in all_sends[q]:
             c.start()
 
+    def wait_bytes(ref, sem):
+        pltpu.make_async_copy(ref, ref, sem).wait()
+
     def receive(q):
-        for d in range(6):
-            to_near(part(senders[d], q, d), q, d).wait_recv()
-
-    load_pls.wait()
-    s2v[...] = jnp.exp(-2.0 * pv[...])
-    total_ls = jnp.sum(pv[...], axis=1, keepdims=True)
+        wait_bytes(gbuf.at[pl.ds(0, 3), q] if q < 2 else cbuf.at[pl.ds(0, 3)], g_recv.at[q])
+
+    wait_bytes(row, in_sem.at[0])
+    s2v[...] = jnp.exp(-2.0 * row[0])
+    total_ls = jnp.sum(row[0], axis=1, keepdims=True)
     acc_sq[...] = jnp.zeros_like(acc_sq)
-    load_w0[0].wait()
-    def half_gram(k):
+    load_first[0].wait()
+    def part_gram(k):
         def body():
             parts = [None, None]
-            first, last = k * (chunks // 2), (k + 1) * (chunks // 2)
+            first, last = cuts[k], cuts[k + 1]
             scale(0, first)
             scale(0, first + 1)
             for c in range(first, last):
@@ -150,15 +170,19 @@
                     scale(0, c + 2)
             both = parts[0] + parts[1]
             if k == 0:
-                g_half[...] = both
+                g_part[...] = both
+            elif k == 1:
+                g_part[...] += both
             else:
-                gbuf[color, 0] = (0.5 * (g_half[...] + both)).astype(BF16)
+                gbuf[color, 0] = (0.5 * (g_part[...] + both)).astype(BF16)
 
         block(body)
 
-    half_gram(0)
-    load_w0[1].wait()
-    half_gram(1)
+    part_gram(0)
+    load_first[1].wait()
+    part_gram(1)
+    load_first[2].wait()
+    part_gram(2)
     for c in load_in:
         c.wait()
     pl.semaphore_wait(barrier, 10)
@@ -175,59 +199,71 @@
     send(0)
     for other in line["y"]:
         pl.semaphore_signal(plane_sem, inc=1, device_id=(other, t), device_id_type=MESH)
-    load_b.wait()
     load_img.wait()
 
     @block
     def _():
         parts = [None, None]
-        differences(0)
-        differences(1)
-        for c in range(chunks):
-            cols = piece(c)
-            parts[c % 2] = plus(parts[c % 2], nt(wv[0, :, cols], dv[:, cols]))
-            if c + 2 < chunks:
-                differences(c + 2)
+        lead = 2
+        for q in range(lead):
+            differences(q)
+        for q in range(2 * chunks):
+            cols = slice(q * 256, (q + 1) * 256)
+            parts[q % 2] = plus(parts[q % 2], nt(wv[0, :, cols], dv[:, cols]))
+            if q + lead < 2 * chunks:
+                differences(q + lead)
+            if q % 5 == 2 and q // 5 < 4:
+                project(t, (q // 5) * 128)
         both = parts[0] + parts[1]
         cbuf[color] = both[:, 0:128] + both[:, 128:256]
 
     send(2)
-    for c in load_lat:
-        c.wait()
+    wait_bytes(nz, in_sem.at[7])
     load_w[0].wait()
 
-    @block
-    def _():
-        mean_t = em[...].T
-        ls_t = el[...].T
-        exp_t = jnp.exp(ls_t)
-        ls_sum = jnp.sum(ls_t, axis=0, keepdims=True)
-        first_row = lax.broadcasted_iota(jnp.int32, (128, 1024), 0) == 0
-        lat[128:256, :] = jnp.where(first_row, 1.0, 0.0).astype(BF16)
+
+    @block
+    def _():
         parts = [None, None]
         for c in range(chunks):
             cols = piece(c)
             parts[c % 2] = plus(parts[c % 2], nt(ws[0, :, cols], wv[1, :, cols]))
-            if c < 8:
-                n_t = nz[pl.ds(c, 128, stride=8), :].T
+            if c == 0:
+                mean_t = nz[samples_n : samples_n + images_n, :].T
+                ls_t = nz[samples_n + images_n :, :].T
+                exp_t = jnp.exp(ls_t)
+                ls_sum = jnp.sum(ls_t, axis=0, keepdims=True)
+                first_row = lax.broadcasted_iota(jnp.int32, (128, 1024), 0) == 0
+                lat[128:256, :] = jnp.where(first_row, 1.0, 0.0).astype(BF16)
+            elif c < 9:
+                i = c - 1
+                n_t = nz[pl.ds(i, 128, stride=8), :].T
                 l_t = mean_t + exp_t * n_t
-                lat[0:128, c * 128 : (c + 1) * 128] = l_t.astype(BF16)
-                squares = jnp.sum(n_t * n_t - l_t * l_t, axis=0, keepdims=True)
-                pp[c : c + 1, :] = 0.5 * squares + ls_sum
+                lat[0:128, i * 128 : (i + 1) * 128] = l_t.astype(BF16)
+                total = jnp.sum(n_t * n_t - l_t * l_t, axis=0, keepdims=True)
+                pp[i : i + 1, :] = 0.5 * total + ls_sum
+            else:
+                squares(c)
         gbuf[color, 1] = (parts[0] + parts[1]).astype(BF16)
 
-    send(1)
+    pl.when(t == 0)(functools.partial(send, 1))
     pl.semaphore_wait(plane_sem, 3)
     for other in line["z"]:
         pl.semaphore_signal(cube_sem, inc=1, device_id=(other, t), device_id_type=MESH)
+    def hide(k):
+        for j in range(2):
+            rows = slice(j * 256, (j + 1) * 256)
+            pre = jnp.dot(wat[k, rows, :], lat[...], preferred_element_type=F32)
+            hid[2 * k + j] = jnp.maximum(pre, 0.0).astype(BF16)
+
+    block(functools.partial(hide, t))
+    pl.when(t == 1)(functools.partial(send, 1))
+    wait_bytes(wv.at[pl.ds(2, 2)], in_sem.at[9])
     pair_copy(wbuf.at[1 - t], 0).wait_recv()
     pair_copy(bbuf.at[1 - t], 1).wait_recv()
-    load_w[1].wait()
-    load_w[2].wait()
-
-    @block
-    def _():
-        row0 = lax.broadcasted_iota(jnp.int32, (128, 128), 0) == 0
+
+    @block
+    def _():
         l0 = l1 = None
         scale(1, 0)
         for c in range(chunks):
@@ -236,22 +272,15 @@
             l1 = plus(l1, nt(ws[1, :, cols], wv[3, :, cols]))
             if c + 1 < chunks:
                 scale(1, c + 1)
-            if c < 8:
-                k, lo = c // 4, (c % 4) * 128
-                rows = slice(c * 128, (c + 1) * 128)
-                wat[rows, 0:128] = wbuf[k, :, lo : lo + 128].astype(F32).T.astype(BF16)
-                bias = jnp.where(row0, bbuf[k, :, lo : lo + 128].astype(F32), 0.0)
-                wat[rows, 128:256] = bias.T.astype(BF16)
+            if c < 4:
+                project(1 - t, c * 128)
+            if c < 9:
+                squares(c)
         lbuf[0] = l0.astype(BF16)
         lbuf[1] = l1.astype(BF16)
 
-    @block
-    def _():
-        for k in range(4):
-            rows = slice(k * 256, (k + 1) * 256)
-            pre = jnp.dot(wat[rows, :], lat[...], preferred_element_type=F32)
-            hid[k] = jnp.maximum(pre, 0.0).astype(BF16)
-
+
+    block(functools.partial(hide, 1 - t))
 
     def against(ref, k, cols):
         return jnp.dot(ref, hid[own[k], :, cols], preferred_element_type=F32)
@@ -286,8 +315,8 @@
 
     image_part = -0.5 * jnp.sum(acc_sq[...].T, axis=0, keepdims=True)
     lsend[8:16, :] = jnp.broadcast_to(image_part - total_ls - pixels * HALF_LOG_TAU, (8, 128))
-    for q in (0, 2, 1):
-        receive(q)
+    receive(0)
+    receive(2)
 
     @block
     def _():
@@ -295,10 +324,20 @@
             cols = slice(n * 256, (n + 1) * 256)
             total = None
             for k in (1, 2, 3):
-                c = own[k]
-                y = against(gbuf[c, 0], k, cols) + against(gbuf[c, 1], (k + 1) % 4, cols)
-                total = plus(total, weigh(y, k, cols))
+                total = plus(total, weigh(against(gbuf[own[k], 0], k, cols), k, cols))
             rows_of(total, n, False)
+
+    receive(1)
+
+    @block
+    def _():
+        for n in range(4):
+            cols = slice(n * 256, (n + 1) * 256)
+            total = None
+            for k in (1, 2, 3):
+                y = against(gbuf[own[k], 1], (k + 1) % 4, cols) * hid[own[k], :, cols].astype(F32)
+                total = plus(total, jnp.sum(y, axis=0, keepdims=True))
+            rows_of(-total, n, False)
 
     share = pltpu.make_async_remote_copy(
         src_ref=lsend, dst_ref=lrecv, send_sem=pair_send.at[2], recv_sem=pair_recv.at[2],
@@ -336,14 +375,18 @@
     pltpu.make_async_copy(others, others, x_send).wait()
     for c in [share, weights, biases]:
         c.wait_send()
-    for q in range(3):
-        for c in all_sends[q]:
-            c.wait_send()
-
-
-def finish(out_ref, bound_ref, lw_ref):
-    bound_ref[...] = out_ref[8:9, :]
-    lw_ref[...] = out_ref[0:8, :]
+    wait_bytes(ws.at[0, pl.ds(0, 96), :], g_send)
+
+
+def finish(out_ref, bound_ref, lw_ref, sems):
+    copies = [
+        pltpu.make_async_copy(out_ref.at[pl.ds(0, 8), :], lw_ref, sems.at[0]),
+        pltpu.make_async_copy(out_ref.at[pl.ds(8, 1), :], bound_ref, sems.at[1]),
+    ]
+    for c in copies:
+        c.start()
+    for c in copies:
+        c.wait()
 
 
 def on_device(images, enc_mean, enc_logscale, noise, w_in, b_in, w_out, b_out, pixel_logscale):
@@ -360,15 +403,15 @@
         out_specs=pl.BlockSpec(memory_space=pltpu.VMEM),
         scratch_shapes=[
             V((4, height, pixels), BF16), V((2, height, pixels), BF16), V((image_count, pixels), BF16),
-            V((2 * image_count, pixels), BF16), V((1, pixels), F32), V((1, pixels), F32),
-            V(noise.shape, F32), V((image_count, latent_dims), F32), V((image_count, latent_dims), F32),
-            V((2, latent_dims, half), BF16), V((2, 1, half), BF16), V((hidden, 256), BF16),
+            V((2 * image_count, pixels), BF16), V((2, 1, pixels), F32),
+            V((noise.shape[0] + 2 * image_count, latent_dims), F32),
+            V((2, latent_dims, half), BF16), V((2, 1, half), BF16), V((2, half, 256), BF16),
             V((256, image_count * sample_count), BF16), V((4, height, image_count * sample_count), BF16),
             V((4, 2, height, height), BF16), V((4, height, image_count), F32), V((2, height, height), BF16),
             V((height, height), F32), V((1, pixels), F32), V((image_count, 128), F32), V((sample_count, image_count), F32),
             V((16, image_count), F32), V((16, image_count), F32),
             V((2, image_count), F32), V((64, 2, image_count), F32),
-            pltpu.SemaphoreType.DMA((13,)), pltpu.SemaphoreType.DMA((3, 6)), pltpu.SemaphoreType.DMA((3, 6)),
+            pltpu.SemaphoreType.DMA((10,)), pltpu.SemaphoreType.DMA, pltpu.SemaphoreType.DMA((3,)),
             pltpu.SemaphoreType.DMA((3,)), pltpu.SemaphoreType.DMA((3,)),
             pltpu.SemaphoreType.DMA, pltpu.SemaphoreType.DMA,
             pltpu.SemaphoreType.REGULAR, pltpu.SemaphoreType.REGULAR,
@@ -384,7 +427,8 @@
             jax.ShapeDtypeStruct((sample_count, image_count), F32),
         ),
         in_specs=[pl.BlockSpec(memory_space=pltpu.VMEM)],
-        out_specs=[pl.BlockSpec(memory_space=pltpu.VMEM)] * 2,
+        out_specs=[pl.BlockSpec(memory_space=pl.ANY)] * 2,
+        scratch_shapes=[pltpu.SemaphoreType.DMA((2,))],
     )(pltpu.with_memory_space_constraint(outputs, pltpu.VMEM))
     return bound.reshape(image_count), lw.T
 

time: 24.8 us -> 24 us (0.968)
  Pallas kernels: 24 us -> 23.3 us
    pallas_call x1, Pallas kernels: 23.4 us -> 22.6 us  [on_device(): pl.pallas_call(kernel, out_shape=FINAL((16, image_count), F32), in_specs=...]
where the time goes in v5:
time: 24 us; the launch traced here: 23.9 us
  Pallas kernels  23.3 us (97%)
  between operations  0.64 us (3%)
    pallas_call x1, Pallas kernels, on_device(): pl.pallas_call(kernel, out_shape=FINAL((16, image_count), F32), in_specs=...  22.6 us
    pallas_call x1, Pallas kernels, on_device(): pl.pallas_call(finish, out_shape=(jax.ShapeDtypeStruct((1, image_count),...  0.61 us

profile of v5, /device:TPU:1, one launch (start us, length us, event | category | flops | bytes accessed | tf_op | source)
XLA Modules:
  0.0 23.9 jit_solution(14631059183294642504)
XLA Ops:
  0.6 22.6 %shard_map.104.out_ref = f32[16,128]{1,0:T(8,128)S(1)} custom-call(bf16[128,6144]{1,0:T(8,128)(2,1)} %images.1, f32[128,128]{1,0:T(8,128)} %enc_mean.1, f32[128,128]{1,0:T(8,128)} %enc_ls.1, f32[1024,128]{1,0:T(8,128)} %bitcast.3, bf16[128,512]{1,0:T(8,128)(2,1)} %w_in.1, bf16[1,512]{1,0:T(2,128)(2,1)} %b_in.1, bf16[1024,6144]{1,0:T(8,128)(2,1)} %w_out.1, ...), custom_call_target="tpu_custom_call" | custom-call | tf_op jit(solution)/shard_map/pallas_call | solution.py:399
  23.3 0.6 %shard_map.105 = (f32[1,128]{1,0:T(1,128)}, f32[8,128]{1,0:T(8,128)}) custom-call(f32[16,128]{1,0:T(8,128)S(1)} %shard_map.104.out_ref), custom_call_target="tpu_custom_call" | custom-call | tf_op jit(solution)/shard_map/pallas_call | solution.py:423
